TPU v7x, 256 devices: a whole 4x4x8 slice. The times are simulated.
256 devices in a mesh: grp: 4 (over x_lo, core), seq: 64 (over y, x_hi, z).
Axes of the slice: x: 4 (x_hi: 2, x_lo: 2; x = x_hi * 2 + x_lo), y: 4, z: 8, core: 2. Of those that a mesh axis runs over, the one named last changes fastest.
Arguments:
- signal: bfloat16 [4, 8192, 2048], P('grp', 'seq'), may hold values from -6 to 6
- gate_in: bfloat16 [4, 8192, 2048], P('grp', 'seq'), may hold values from -6 to 6
- gate_out: bfloat16 [4, 8192, 2048], P('grp', 'seq'), may hold values from -6 to 6
- pos_weight: float32 [33, 64], replicated, may hold values from -1 to 1
- pos_bias: float32 [64], replicated, may hold values from -1 to 1
- inner_weight: float32 [2, 64, 64], replicated, may hold values from -0.75 to 0.75
- inner_bias: float32 [2, 64], replicated, may hold values from -1 to 1
- frequency: float32 [64], replicated, may hold values from 1 to 12
- out_weight: float32 [64, 2048], replicated, may hold values from -0.75 to 0.75
- decay_rates: float32 [2048], replicated, may hold values from 0.3 to 3000
- skip_gain: float32 [2048], replicated, may hold values from -6 to 6
Outputs:
- layer_out: bfloat16 [4, 8192, 2048], P('grp', 'seq')
All inputs are finite; a program needn't handle non-finite values.
Results may differ from a plain program's by a relative error of at most 0.009.
Values may be sent and summed in bfloat16 or wider, within the bound.
No kernel may reach another device: no remote copies, remote signals or barrier semaphores. Data moves between devices by JAX's collectives and lax.ppermute only.
A program may use at most 64 MiB of HBM per device.

v0:
```python
import jax
import jax.numpy as jnp
from jax import lax
from jax.sharding import PartitionSpec as P

TWO_PI = 6.283185307179586
FLOOR_SHIFT = 0.05
EPSILON = 1e-06
HIGHEST = lax.Precision.HIGHEST


def sent_to_all(shard, axis):
    peers = lax.axis_size(axis)
    return lax.all_to_all(
        jnp.broadcast_to(shard[None], (peers, *shard.shape)), axis, 0, 0, tiled=True
    )


def over_copies(shard, axis):
    everything = sent_to_all(shard, axis)
    return jnp.sum(everything, axis=0)


def in_one_piece(arrays, axis, split_dim, concat_dim, along):
    both = jnp.concatenate(arrays, axis=along)
    whole, at, finished = (
        lax.all_to_all(both, axis, split_axis=split_dim, concat_axis=concat_dim, tiled=True),
        0,
        [],
    )
    for a in arrays:
        finished.append(lax.slice_in_dim(whole, at, at + a.shape[along], axis=along))
        at += a.shape[along]
    return tuple(finished)


def unit_angle(index, period):
    return (index % period).astype(jnp.float32) * (TWO_PI / period)


def section_tables(row_ids, col_ids, period):
    angle = unit_angle(row_ids[:, None] * col_ids[None, :], period)
    return (jnp.cos(angle).astype(jnp.bfloat16), jnp.sin(angle).astype(jnp.bfloat16))


def filter_hidden(positions, total, pos_weight, pos_bias, inner_weight, inner_bias, frequency):
    band_count = (pos_weight.shape[0] - 1) // 2
    position_f = positions.astype(jnp.float32)
    moments = position_f / (total - 1)
    phases = position_f * (TWO_PI / total)
    tone_list = jnp.linspace(0.0001, band_count - 1, band_count).astype(jnp.float32)
    angles = tone_list[:, None] * phases[None, :]
    features = jnp.concatenate([moments[None, :], jnp.cos(angles), -jnp.sin(angles)], axis=0)
    hidden = jnp.sin(
        frequency[:, None]
        * (jnp.dot(pos_weight.T, features, precision=HIGHEST) + pos_bias[:, None])
    )
    for layer_index in range(inner_weight.shape[0]):
        hidden = jnp.sin(
            frequency[:, None]
            * (
                jnp.dot(inner_weight[layer_index].T, hidden, precision=HIGHEST)
                + inner_bias[layer_index][:, None]
            )
        )
    return (hidden, moments)


def filter_rows(
    positions,
    total,
    pos_weight,
    pos_bias,
    inner_weight,
    inner_bias,
    frequency,
    out_weight,
    decay_rates,
):
    hidden, moments = filter_hidden(
        positions, total, pos_weight, pos_bias, inner_weight, inner_bias, frequency
    )
    shaped = lax.dot_general(hidden, out_weight, (((0,), (0,)), ((), ())), precision=HIGHEST)
    return shaped * (jnp.exp(-moments[:, None] * decay_rates[None, :]) + FLOOR_SHIFT)


def per_device(
    signal,
    gate_in,
    gate_out,
    pos_weight,
    pos_bias,
    inner_weight,
    inner_bias,
    frequency,
    out_weight,
    decay_rates,
    skip_gain,
):
    blocks = lax.axis_size("seq")
    block_id = lax.axis_index("seq")
    span = signal.shape[1]
    per_block = span // blocks
    rows_freq = 2 * blocks
    length = span * blocks
    period = 2 * length
    gated = (gate_in[0].astype(jnp.float32) * signal[0].astype(jnp.float32)).astype(jnp.bfloat16)
    fwd_cos, fwd_sin = section_tables(
        jnp.arange(rows_freq, dtype=jnp.int32), jnp.arange(blocks, dtype=jnp.int32), rows_freq
    )
    back_cos, back_sin = section_tables(
        jnp.arange(blocks, dtype=jnp.int32), jnp.arange(rows_freq, dtype=jnp.int32), rows_freq
    )
    column_ids = jnp.arange(span, dtype=jnp.int32)
    positions = block_id * span + column_ids
    shaped = filter_rows(
        positions,
        length,
        pos_weight,
        pos_bias,
        inner_weight,
        inner_bias,
        frequency,
        out_weight,
        decay_rates,
    )
    totals = over_copies(jnp.sum(shaped * shaped, axis=0), "seq")
    scale = lax.rsqrt(totals + EPSILON)
    filter_taps = shaped.astype(jnp.bfloat16)
    gathered_data, gathered_taps = in_one_piece((gated[None], filter_taps[None]), "seq", 1, 0, 2)

    def first_section(source):
        channels = source.shape[2]
        flat = source.reshape(blocks, per_block * channels)
        real_part = jnp.dot(fwd_cos, flat, preferred_element_type=jnp.float32).astype(jnp.bfloat16)
        imag_part = (-jnp.dot(fwd_sin, flat, preferred_element_type=jnp.float32)).astype(
            jnp.bfloat16
        )
        return (
            real_part.reshape(rows_freq, per_block, channels),
            imag_part.reshape(rows_freq, per_block, channels),
        )

    own_rows = 2 * block_id + jnp.arange(2, dtype=jnp.int32)
    wave_ids = own_rows[:, None] + rows_freq * column_ids[None, :]
    angle = unit_angle(wave_ids[:, :, None] * column_ids[None, None, :], period)
    cosines = jnp.cos(angle).astype(jnp.bfloat16)
    sines = jnp.sin(angle).astype(jnp.bfloat16)
    forward_stack = jnp.concatenate([cosines, sines], axis=1)
    backward_stack = jnp.concatenate(
        [jnp.swapaxes(cosines, 1, 2), jnp.swapaxes(sines, 1, 2)], axis=1
    )

    def forward_rows(part_real, part_imag):
        with_real = jnp.einsum(
            "rkb,rbc->rkc", forward_stack, part_real, preferred_element_type=jnp.float32
        )
        with_imag = jnp.einsum(
            "rkb,rbc->rkc", forward_stack, part_imag, preferred_element_type=jnp.float32
        )
        return (
            with_real[:, :span] + with_imag[:, span:],
            with_imag[:, :span] - with_real[:, span:],
        )

    data_real, data_imag = first_section(gathered_data)
    taps_real, taps_imag = first_section(gathered_taps)
    pieces = (
        lax.all_to_all(data_real, "seq", split_axis=0, concat_axis=1, tiled=True),
        lax.all_to_all(data_imag, "seq", split_axis=0, concat_axis=1, tiled=True),
        lax.all_to_all(taps_real, "seq", split_axis=0, concat_axis=1, tiled=True),
        lax.all_to_all(taps_imag, "seq", split_axis=0, concat_axis=1, tiled=True),
    )
    first_real, first_imag = forward_rows(pieces[0], pieces[1])
    spec_real, spec_imag = forward_rows(pieces[2], pieces[3])
    filter_real = spec_real.astype(jnp.bfloat16)
    filter_imag = spec_imag.astype(jnp.bfloat16)
    filt_real = filter_real.astype(jnp.float32)
    filt_imag = filter_imag.astype(jnp.float32)
    prod_real = ((first_real * filt_real - first_imag * filt_imag) * scale).astype(jnp.bfloat16)
    prod_imag = ((first_real * filt_imag + first_imag * filt_real) * scale).astype(jnp.bfloat16)
    with_real = jnp.einsum(
        "rkb,rbc->rkc", backward_stack, prod_real, preferred_element_type=jnp.float32
    )
    with_imag = jnp.einsum(
        "rkb,rbc->rkc", backward_stack, prod_imag, preferred_element_type=jnp.float32
    )
    back_real = (with_real[:, :span] - with_imag[:, span:]).astype(jnp.bfloat16)
    back_imag = (with_imag[:, :span] + with_real[:, span:]).astype(jnp.bfloat16)
    pieces = (
        lax.all_to_all(back_real, "seq", split_axis=1, concat_axis=0, tiled=True),
        lax.all_to_all(back_imag, "seq", split_axis=1, concat_axis=0, tiled=True),
    )
    channels = pieces[0].shape[2]
    flat_real = pieces[0].reshape(rows_freq, per_block * channels)
    flat_imag = pieces[1].reshape(rows_freq, per_block * channels)
    convolved = (
        jnp.dot(back_cos, flat_real, preferred_element_type=jnp.float32)
        - jnp.dot(back_sin, flat_imag, preferred_element_type=jnp.float32)
    ) * (1.0 / period)
    convolved_rows = lax.all_to_all(
        convolved.reshape(blocks, per_block, channels).astype(jnp.bfloat16),
        "seq",
        split_axis=0,
        concat_axis=1,
        tiled=True,
    ).astype(jnp.float32)[0]
    mixed = gate_out[0].astype(jnp.float32) * (
        convolved_rows + skip_gain[None, :] * gated.astype(jnp.float32)
    )
    return mixed.astype(jnp.bfloat16)[None]


def solution(mesh):
    return jax.shard_map(
        per_device,
        mesh=mesh,
        in_specs=(
            P("grp", "seq", None),
            P("grp", "seq", None),
            P("grp", "seq", None),
            P(),
            P(),
            P(),
            P(),
            P(),
            P(),
            P(),
            P(),
        ),
        out_specs=P("grp", "seq", None),
        check_vma=False,
    )
```

profile of v0, /device:TPU:32, one launch (start us, length us, event | category | flops | bytes accessed | tf_op | source)
XLA Modules:
  0.0 357.4 jit_solution(10181429200125694032)
XLA Ops:
  7.0 2.4 copy.74
  9.9 8.0 %reduce.3 = bf16[128,4096]{1,0:T(8,128)(2,1)} reduce(bf16[128,1,4096]{2,1,0:T(2,128)(2,1)S(1)} %bitcast.62, bf16[]{:T(256)} %broadcast.146), dimensions={1}, to_apply=%bitcast.61.reduce_sub_computation | reduce | bytes 2097154
  17.9 1.7 reshape.149
  19.7 56.8 %all_to_all.129 = bf16[64,2,4096]{2,1,0:T(2,128)(2,1)} all-to-all(bf16[64,2,4096]{2,1,0:T(2,128)(2,1)S(1)} %reshape.149), channel_id=1, replica_groups=mesh['grp'=4,'seq'=64] {'seq'}, dimensions={0} | all-to-all | bytes 2097152 | tf_op jit(solution)/shard_map/all_to_all | solution.py:27
  77.5 6.1 %all-to-all-start.5 = ((f32[64,1,2048]{2,1,0:T(1,128)}), f32[64,1,2048]{2,1,0:T(1,128)}, u32[]{:S(2)}, u32[]{:S(2)}) async-start(f32[64,1,2048]{2,1,0:T(1,128)} %broadcast_in_dim.7), calls=%async_computation.5 | async-start | bytes 1048576 | tf_op jit(solution)/shard_map/all_to_all | solution.py:14
  83.6 6.5 %reshape.150 = bf16[128,1,4096]{2,1,0:T(2,128)(2,1)S(1)} reshape(bf16[64,2,4096]{2,1,0:T(2,128)(2,1)} %all_to_all.129) | data formatting | bytes 2097152
  90.1 7.2 %bitcast_reduce_fusion = bf16[128,4096]{1,0:T(8,128)(2,1)} fusion(bf16[128,1,4096]{2,1,0:T(2,128)(2,1)S(1)} %reshape.150), kind=kLoop, calls=%fused_computation.158 | loop fusion | bytes 2097152 | tf_op jit(solution)/shard_map/all_to_all | solution.py:27
  97.3 1.7 all_to_all.95
  103.0 12.8 %all-to-all-start.4 = ((bf16[128,2,2048]{2,1,0:T(2,128)(2,1)}), bf16[128,2,2048]{2,1,0:T(2,128)(2,1)S(1)}, u32[]{:S(2)}, u32[]{:S(2)}) async-start(bf16[128,2,2048]{2,1,0:T(2,128)(2,1)} %reshape.144), calls=%async_computation.4 | async-start | bytes 2097152 | tf_op jit(solution)/shard_map/all_to_all | solution.py:172
  118.0 27.2 %all-to-all-done.4 = bf16[128,2,2048]{2,1,0:T(2,128)(2,1)S(1)} async-done(((bf16[128,2,2048]{2,1,0:T(2,128)(2,1)}), bf16[128,2,2048]{2,1,0:T(2,128)(2,1)S(1)}, u32[]{:S(2)}, u32[]{:S(2)}) %all-to-all-start.4) | async-done | bytes 1048608 | tf_op jit(solution)/shard_map/all_to_all | solution.py:172
  145.2 5.8 %all-to-all-start.3 = ((bf16[128,2,2048]{2,1,0:T(2,128)(2,1)}), bf16[128,2,2048]{2,1,0:T(2,128)(2,1)S(1)}, u32[]{:S(2)}, u32[]{:S(2)}) async-start(bf16[128,2,2048]{2,1,0:T(2,128)(2,1)} %reshape.143), calls=%async_computation.3 | async-start | bytes 2097152 | tf_op jit(solution)/shard_map/all_to_all | solution.py:171
  153.8 2.6 reshape.141
  156.4 23.4 %all-to-all-done.3 = bf16[128,2,2048]{2,1,0:T(2,128)(2,1)S(1)} async-done(((bf16[128,2,2048]{2,1,0:T(2,128)(2,1)}), bf16[128,2,2048]{2,1,0:T(2,128)(2,1)S(1)}, u32[]{:S(2)}, u32[]{:S(2)}) %all-to-all-start.3) | async-done | bytes 1048608 | tf_op jit(solution)/shard_map/all_to_all | solution.py:171
  179.9 5.9 %all-to-all-start.2 = ((bf16[128,2,2048]{2,1,0:T(2,128)(2,1)}), bf16[128,2,2048]{2,1,0:T(2,128)(2,1)}, u32[]{:S(2)}, u32[]{:S(2)}) async-start(bf16[128,2,2048]{2,1,0:T(2,128)(2,1)} %reshape.141), calls=%async_computation.2 | async-start | bytes 2097152 | tf_op jit(solution)/shard_map/all_to_all | solution.py:170
  187.4 2.6 reshape.140
  190.0 24.5 %all-to-all-done.2 = bf16[128,2,2048]{2,1,0:T(2,128)(2,1)} async-done(((bf16[128,2,2048]{2,1,0:T(2,128)(2,1)}), bf16[128,2,2048]{2,1,0:T(2,128)(2,1)}, u32[]{:S(2)}, u32[]{:S(2)}) %all-to-all-start.2) | async-done | bytes 1048608 | tf_op jit(solution)/shard_map/all_to_all | solution.py:170
  214.5 6.5 %all-to-all-start.1 = ((bf16[128,2,2048]{2,1,0:T(2,128)(2,1)}), bf16[128,2,2048]{2,1,0:T(2,128)(2,1)}, u32[]{:S(2)}, u32[]{:S(2)}) async-start(bf16[128,2,2048]{2,1,0:T(2,128)(2,1)} %reshape.140), calls=%async_computation.1 | async-start | bytes 2097152 | tf_op jit(solution)/shard_map/all_to_all | solution.py:169
  225.3 2.3 all_to_all.111
  229.5 2.0 copy.72
  232.8 2.6 fusion.92
  235.5 2.7 fusion.93
  238.2 2.7 fusion.94
  240.8 8.4 %all-to-all-done.1 = bf16[128,2,2048]{2,1,0:T(2,128)(2,1)} async-done(((bf16[128,2,2048]{2,1,0:T(2,128)(2,1)}), bf16[128,2,2048]{2,1,0:T(2,128)(2,1)}, u32[]{:S(2)}, u32[]{:S(2)}) %all-to-all-start.1) | async-done | bytes 1048608 | tf_op jit(solution)/shard_map/all_to_all | solution.py:169
  249.2 1.9 copy.73
  253.8 3.0 fusion.12
  260.0 2.1 copy.55
  262.0 5.9 %all-to-all-start.6 = ((bf16[2,128,2048]{2,0,1:T(2,128)(2,1)}), bf16[2,128,2048]{2,0,1:T(2,128)(2,1)S(1)}, u32[]{:S(2)}, u32[]{:S(2)}) async-start(bf16[2,128,2048]{2,0,1:T(2,128)(2,1)} %copy.55), calls=%async_computation.6 | async-start | bytes 2097152 | tf_op jit(solution)/shard_map/all_to_all | solution.py:191
  268.0 2.1 copy.57
  270.0 26.3 %all-to-all-done.6 = bf16[2,128,2048]{2,0,1:T(2,128)(2,1)S(1)} async-done(((bf16[2,128,2048]{2,0,1:T(2,128)(2,1)}), bf16[2,128,2048]{2,0,1:T(2,128)(2,1)S(1)}, u32[]{:S(2)}, u32[]{:S(2)}) %all-to-all-start.6) | async-done | bytes 1048608 | tf_op jit(solution)/shard_map/all_to_all | solution.py:191
  296.4 5.8 %all-to-all-start.7 = ((bf16[2,128,2048]{2,0,1:T(2,128)(2,1)}), bf16[2,128,2048]{2,0,1:T(2,128)(2,1)S(1)}, u32[]{:S(2)}, u32[]{:S(2)}) async-start(bf16[2,128,2048]{2,0,1:T(2,128)(2,1)} %copy.57), calls=%async_computation.7 | async-start | bytes 2097152 | tf_op jit(solution)/shard_map/all_to_all | solution.py:192
  304.0 26.6 %all-to-all-done.7 = bf16[2,128,2048]{2,0,1:T(2,128)(2,1)S(1)} async-done(((bf16[2,128,2048]{2,0,1:T(2,128)(2,1)}), bf16[2,128,2048]{2,0,1:T(2,128)(2,1)S(1)}, u32[]{:S(2)}, u32[]{:S(2)}) %all-to-all-start.7) | async-done | bytes 1048608 | tf_op jit(solution)/shard_map/all_to_all | solution.py:192
  332.9 23.2 %all_to_all.130 = bf16[64,2,2048]{2,1,0:T(2,128)(2,1)S(1)} all-to-all(bf16[64,2,2048]{2,1,0:T(2,128)(2,1)S(1)} %convert_element_type.190), channel_id=1, replica_groups=mesh['grp'=4,'seq'=64] {'seq'}, dimensions={0} | all-to-all | bytes 1048576 | tf_op jit(solution)/shard_map/all_to_all | solution.py:201
  (68 shorter events, 37.8 us)
Async XLA Ops:
  0.0 5.7 %copy-start = (f32[64,2048]{1,0:T(8,128)S(1)}, f32[64,2048]{1,0:T(8,128)}, u32[]{:S(2)}) copy-start(f32[64,2048]{1,0:T(8,128)} %param.19) | copy-start | bytes 1572868
  0.0 5.7 %copy-start.9 = (f32[2048]{0:T(1024)S(1)}, f32[2048]{0:T(1024)}, u32[]{:S(2)}) copy-start(f32[2048]{0:T(1024)} %param.20) | copy-start | bytes 24580
  77.5 25.5 %all-to-all-start.5 = ((f32[64,1,2048]{2,1,0:T(1,128)}), f32[64,1,2048]{2,1,0:T(1,128)}, u32[]{:S(2)}, u32[]{:S(2)}) async-start(f32[64,1,2048]{2,1,0:T(1,128)} %broadcast_in_dim.7), calls=%async_computation.5 | async-start | bytes 1048576 | tf_op jit(solution)/shard_map/all_to_all | solution.py:14
  103.0 42.2 %all-to-all-start.4 = ((bf16[128,2,2048]{2,1,0:T(2,128)(2,1)}), bf16[128,2,2048]{2,1,0:T(2,128)(2,1)S(1)}, u32[]{:S(2)}, u32[]{:S(2)}) async-start(bf16[128,2,2048]{2,1,0:T(2,128)(2,1)} %reshape.144), calls=%async_computation.4 | async-start | bytes 2097152 | tf_op jit(solution)/shard_map/all_to_all | solution.py:172
  145.2 34.7 %all-to-all-start.3 = ((bf16[128,2,2048]{2,1,0:T(2,128)(2,1)}), bf16[128,2,2048]{2,1,0:T(2,128)(2,1)S(1)}, u32[]{:S(2)}, u32[]{:S(2)}) async-start(bf16[128,2,2048]{2,1,0:T(2,128)(2,1)} %reshape.143), calls=%async_computation.3 | async-start | bytes 2097152 | tf_op jit(solution)/shard_map/all_to_all | solution.py:171
  179.9 34.6 %all-to-all-start.2 = ((bf16[128,2,2048]{2,1,0:T(2,128)(2,1)}), bf16[128,2,2048]{2,1,0:T(2,128)(2,1)}, u32[]{:S(2)}, u32[]{:S(2)}) async-start(bf16[128,2,2048]{2,1,0:T(2,128)(2,1)} %reshape.141), calls=%async_computation.2 | async-start | bytes 2097152 | tf_op jit(solution)/shard_map/all_to_all | solution.py:170
  214.5 34.7 %all-to-all-start.1 = ((bf16[128,2,2048]{2,1,0:T(2,128)(2,1)}), bf16[128,2,2048]{2,1,0:T(2,128)(2,1)}, u32[]{:S(2)}, u32[]{:S(2)}) async-start(bf16[128,2,2048]{2,1,0:T(2,128)(2,1)} %reshape.140), calls=%async_computation.1 | async-start | bytes 2097152 | tf_op jit(solution)/shard_map/all_to_all | solution.py:169
  229.5 3.3 copy-start.4
  232.8 2.7 copy-start.5
  235.5 2.7 copy-start.6
  251.6 2.2 copy-start.2
  253.8 3.5 copy-start.3
  262.0 34.3 %all-to-all-start.6 = ((bf16[2,128,2048]{2,0,1:T(2,128)(2,1)}), bf16[2,128,2048]{2,0,1:T(2,128)(2,1)S(1)}, u32[]{:S(2)}, u32[]{:S(2)}) async-start(bf16[2,128,2048]{2,0,1:T(2,128)(2,1)} %copy.55), calls=%async_computation.6 | async-start | bytes 2097152 | tf_op jit(solution)/shard_map/all_to_all | solution.py:191
  296.4 34.2 %all-to-all-start.7 = ((bf16[2,128,2048]{2,0,1:T(2,128)(2,1)}), bf16[2,128,2048]{2,0,1:T(2,128)(2,1)S(1)}, u32[]{:S(2)}, u32[]{:S(2)}) async-start(bf16[2,128,2048]{2,0,1:T(2,128)(2,1)} %copy.57), calls=%async_computation.7 | async-start | bytes 2097152 | tf_op jit(solution)/shard_map/all_to_all | solution.py:192
  332.5 23.7 %copy-start.7 = (bf16[1,128,2048]{2,1,0:T(8,128)(2,1)S(1)}, bf16[1,128,2048]{2,1,0:T(8,128)(2,1)}, u32[]{:S(2)}) copy-start(bf16[1,128,2048]{2,1,0:T(8,128)(2,1)} %param.13) | copy-start | bytes 1572868
  332.5 23.7 %copy-start.8 = (f32[2048]{0:T(1024)S(1)}, f32[2048]{0:T(1024)}, u32[]{:S(2)}) copy-start(f32[2048]{0:T(1024)} %param.21) | copy-start | bytes 24580
  332.9 24.3 %copy-start.1 = (f32[64,2048]{1,0:T(8,128)S(1)}, f32[64,2048]{1,0:T(8,128)}, u32[]{:S(2)}) copy-start(f32[64,2048]{1,0:T(8,128)} %param.19) | copy-start | bytes 1572868
where the time goes:
time: 362 us; the launch traced here: 357 us
  waiting for transfers between devices  136 us (38%)
  blocking collectives  80 us (22%)
  local copies, waits for them, and re-layouts  54.5 us (15%)
  starting transfers between devices  48.6 us (13%)
  matrix products  20.3 us (6%)
  other arithmetic  17.2 us (5%)
    all_to_all x1, blocking collectives, in_one_piece(): lax.all_to_all(both, axis, split_axis=split_dim, concat_axis=concat_dim,...  56.8 us
    all_to_all x1, waiting for transfers between devices, per_device(): lax.all_to_all(taps_imag, 'seq', split_axis=0, concat_axis=1, tiled=True)  27.2 us
    all_to_all x1, waiting for transfers between devices, per_device(): lax.all_to_all(back_imag, 'seq', split_axis=1, concat_axis=0, tiled=True)  26.6 us
    all_to_all x1, waiting for transfers between devices, per_device(): lax.all_to_all(back_real, 'seq', split_axis=1, concat_axis=0, tiled=True)  26.3 us
    all_to_all x1, waiting for transfers between devices, per_device(): lax.all_to_all(data_imag, 'seq', split_axis=0, concat_axis=1, tiled=True)  24.5 us
    all_to_all x1, waiting for transfers between devices, per_device(): lax.all_to_all(taps_real, 'seq', split_axis=0, concat_axis=1, tiled=True)  23.4 us
    all_to_all x1, blocking collectives, per_device(): lax.all_to_all(convolved.reshape(blocks, per_block, channels).astype(jnp....  23.2 us
    unnamed x27, local copies, waits for them, and re-layouts  12.9 us
  transfers between devices with their start and end apart: 7, of which 6 were waited for; matrix products, arithmetic and copies ran while one was open for 14% of the time, Pallas kernels for 0%

commit v1 on v0

v1 whole, which is shorter than its diff:
```python
import functools

import jax
import jax.numpy as jnp
import numpy as np
from jax import lax
from jax.experimental import pallas as pl
from jax.experimental.pallas import tpu as pltpu
from jax.sharding import PartitionSpec as P

FLOOR_SHIFT = 0.05
EPSILON = 1e-06
HIGHEST = lax.Precision.HIGHEST
F32 = jnp.float32
BF16 = jnp.bfloat16
SINE = (
    6.283182818534707,
    -41.34142139736154,
    81.5961838429123,
    -76.58010024733522,
    41.20539373944452,
    -12.271260700128162,
)


def sine_of_turns(turns):
    r = turns - jnp.round(turns)
    r2 = r * r
    poly = jnp.full_like(r2, SINE[-1])
    for factor in SINE[-2::-1]:
        poly = poly * r2 + factor
    return poly * r


def transform_tables(blocks, span):
    rows = np.arange(blocks) + 0.5
    turn = 2.0 * np.pi * np.outer(rows, np.arange(blocks)) / (2 * blocks)
    first = np.concatenate([np.cos(turn), -np.sin(turn)], axis=0)
    last = np.concatenate([np.cos(turn.T), -np.sin(turn.T)], axis=1) / (blocks * span)
    bend = 2.0 * np.pi * np.outer(rows, np.arange(span)) / (2 * blocks * span)
    twiddle = np.stack([np.cos(bend), -np.sin(bend)])
    cols = 2.0 * np.pi * (np.outer(np.arange(span), np.arange(span)) % span) / span
    cosines, sines = np.cos(cols), np.sin(cols)
    forward = np.block([[cosines, -sines], [sines, cosines]])
    backward = np.block([[cosines, sines], [-sines, cosines]])
    return (
        jnp.asarray(first, BF16),
        jnp.asarray(last, BF16),
        jnp.asarray(twiddle, F32),
        jnp.asarray(forward, BF16),
        jnp.asarray(backward, BF16),
    )


def gate_kernel(signal_ref, gate_ref, out_ref):
    gated = gate_ref[...].astype(F32) * signal_ref[...].astype(F32)
    out_ref[...] = gated.astype(BF16).T


def spectrum_of(rows_ref, group, count, blocks, channels, first, twiddle_ref, forward):
    span = rows_ref.shape[1]
    taken = [
        rows_ref[pl.ds(group * count + j, blocks, stride=channels), :].astype(BF16)
        for j in range(count)
    ]
    section = jnp.dot(first, jnp.concatenate(taken, axis=1), preferred_element_type=F32)
    cosines, sines = twiddle_ref[0], twiddle_ref[1]
    turned = []
    for j in range(count):
        real = section[:blocks, j * span : (j + 1) * span]
        imag = section[blocks:, j * span : (j + 1) * span]
        turned.append(
            jnp.concatenate(
                [
                    (real * cosines - imag * sines).astype(BF16),
                    (real * sines + imag * cosines).astype(BF16),
                ],
                axis=1,
            )
        )
    return jnp.dot(jnp.concatenate(turned, axis=0), forward, preferred_element_type=F32)


def filter_kernel(
    total,
    count,
    pos_weight_ref,
    columns_ref,
    inner_ref,
    out_weight_ref,
    decay_ref,
    first_ref,
    twiddle_ref,
    forward_ref,
    spec_ref,
    taps_ref,
    square_ref,
):
    channels = out_weight_ref.shape[0]
    span = taps_ref.shape[1]
    blocks = taps_ref.shape[0] // channels
    step_blocks = 8
    width = step_blocks * span
    layers = inner_ref.shape[0]
    bands = (pos_weight_ref.shape[1] - 1) // 2
    frequency = columns_ref[:, 0:1]
    turns_per = frequency * (1.0 / (2.0 * np.pi))
    biases = [columns_ref[:, i + 1 : i + 2] for i in range(layers + 1)]
    weight_time = pos_weight_ref[:, 0:1]
    weight_tone = pos_weight_ref[:, 1:]
    decay = decay_ref[...]
    tone = 0.0001 + lax.broadcasted_iota(jnp.int32, (bands, 1), 0).astype(F32) * (
        (bands - 1 - 0.0001) / (bands - 1)
    )
    square_ref[...] = jnp.zeros_like(square_ref)

    def positions_step(step, carry):
        position = (
            lax.broadcasted_iota(jnp.int32, (1, width), 1) + step * width
        ).astype(F32)
        moment = position / (total - 1)
        angle = tone * (position * (1.0 / total))
        features = jnp.concatenate(
            [sine_of_turns(angle + 0.25), -sine_of_turns(angle)], axis=0
        )
        pre = jnp.dot(weight_tone, features, precision=HIGHEST, preferred_element_type=F32)
        hidden = sine_of_turns(turns_per * (pre + weight_time * moment + biases[0]))
        for i in range(layers):
            pre = jnp.dot(inner_ref[i], hidden, precision=HIGHEST, preferred_element_type=F32)
            hidden = sine_of_turns(turns_per * (pre + biases[i + 1]))
        shaped = jnp.dot(
            out_weight_ref[...], hidden, precision=HIGHEST, preferred_element_type=F32
        )
        raw = shaped * (jnp.exp(-moment * decay) + FLOOR_SHIFT)
        squares = raw * raw
        folded = square_ref[...]
        for j in range(step_blocks):
            folded = folded + squares[:, j * span : (j + 1) * span]
            at = pl.multiple_of((step * step_blocks + j) * channels, channels)
            taps_ref[pl.ds(at, channels), :] = raw[:, j * span : (j + 1) * span]
        square_ref[...] = folded
        return carry

    lax.fori_loop(0, blocks // step_blocks, positions_step, 0)
    summed = jnp.sum(square_ref[...], axis=1, keepdims=True)
    square_ref[...] = jnp.broadcast_to(lax.rsqrt(summed + EPSILON), square_ref.shape)

    def spectrum_step(group, carry):
        spectrum = spectrum_of(
            taps_ref, group, count, blocks, channels, first_ref[...], twiddle_ref, forward_ref[...]
        )
        pieces = []
        for j in range(count):
            scale = square_ref[pl.ds(group * count + j, 1), :]
            scale = jnp.concatenate([scale, scale], axis=1)
            pieces.append((spectrum[j * blocks : (j + 1) * blocks] * scale).astype(BF16))
        spec_ref[group] = jnp.concatenate(pieces, axis=0)
        return carry

    lax.fori_loop(0, channels // count, spectrum_step, 0)


def convolve_kernel(
    count,
    data_ref,
    spec_ref,
    first_ref,
    last_ref,
    twiddle_ref,
    forward_ref,
    backward_ref,
    out_ref,
    rows_ref,
    result_ref,
):
    blocks, channels, span = data_ref.shape
    rows_ref[...] = data_ref[...].astype(F32).reshape(blocks * channels, span)

    def group_step(group, carry):
        spectrum = spectrum_of(
            rows_ref, group, count, blocks, channels, first_ref[...], twiddle_ref, forward_ref[...]
        )
        filt = spec_ref[group].astype(F32)
        real, imag = spectrum[:, :span], spectrum[:, span:]
        filt_real, filt_imag = filt[:, :span], filt[:, span:]
        product = jnp.concatenate(
            [
                (real * filt_real - imag * filt_imag).astype(BF16),
                (real * filt_imag + imag * filt_real).astype(BF16),
            ],
            axis=1,
        )
        back = jnp.dot(product, backward_ref[...], preferred_element_type=F32)
        cosines, sines = twiddle_ref[0], twiddle_ref[1]
        turned = []
        for j in range(count):
            real = back[j * blocks : (j + 1) * blocks, :span]
            imag = back[j * blocks : (j + 1) * blocks, span:]
            turned.append(
                jnp.concatenate(
                    [
                        (real * cosines + imag * sines).astype(BF16),
                        (imag * cosines - real * sines).astype(BF16),
                    ],
                    axis=0,
                )
            )
        convolved = jnp.dot(
            last_ref[...], jnp.concatenate(turned, axis=1), preferred_element_type=F32
        )
        for j in range(count):
            result_ref[pl.ds(group * count + j, blocks, stride=channels), :] = convolved[
                :, j * span : (j + 1) * span
            ]
        return carry

    lax.fori_loop(0, channels // count, group_step, 0)
    out_ref[...] = result_ref[...].reshape(blocks, channels, span).astype(BF16)


def mix_kernel(conv_ref, signal_ref, gate_in_ref, gate_out_ref, skip_ref, out_ref):
    gated = (gate_in_ref[...].astype(F32) * signal_ref[...].astype(F32)).astype(BF16)
    conv = conv_ref[...].T.astype(F32)
    mixed = gate_out_ref[...].astype(F32) * (conv + skip_ref[...] * gated.astype(F32))
    out_ref[...] = mixed.astype(BF16)


def per_device(
    signal,
    gate_in,
    gate_out,
    pos_weight,
    pos_bias,
    inner_weight,
    inner_bias,
    frequency,
    out_weight,
    decay_rates,
    skip_gain,
):
    blocks = lax.axis_size("seq")
    block_id = lax.axis_index("seq")
    span, width = signal.shape[1:]
    channels = width // blocks
    length = blocks * span
    signal, gate_in, gate_out = signal[0], gate_in[0], gate_out[0]
    first, last, twiddle, forward, backward = transform_tables(blocks, span)
    chunk = 512
    count = 4
    groups = channels // count

    natural = pl.BlockSpec((span, chunk), lambda i: (0, i))
    swapped = pl.BlockSpec((chunk, span), lambda i: (i, 0))
    gated = pl.pallas_call(
        gate_kernel,
        grid=(width // chunk,),
        in_specs=[natural, natural],
        out_specs=swapped,
        out_shape=jax.ShapeDtypeStruct((width, span), BF16),
        name="gate",
    )(signal, gate_in)

    arrived = lax.all_to_all(
        gated.reshape(blocks, channels, span), "seq", split_axis=0, concat_axis=0, tiled=True
    )

    own_weight = lax.dynamic_slice_in_dim(out_weight, block_id * channels, channels, axis=1).T
    own_decay = lax.dynamic_slice_in_dim(decay_rates, block_id * channels, channels, axis=0)[:, None]
    columns = jnp.concatenate([frequency[None], pos_bias[None], inner_bias], axis=0).T
    spec = pl.pallas_call(
        functools.partial(filter_kernel, length, count),
        out_shape=jax.ShapeDtypeStruct((groups, count * blocks, 2 * span), BF16),
        scratch_shapes=[
            pltpu.VMEM((blocks * channels, span), F32),
            pltpu.VMEM((channels, span), F32),
        ],
        cost_estimate=pl.CostEstimate(
            flops=20_000_000_000, bytes_accessed=2_000_000, transcendentals=2_000_000
        ),
        name="filter",
    )(
        pos_weight.T,
        columns,
        jnp.swapaxes(inner_weight, 1, 2),
        own_weight,
        own_decay,
        first,
        twiddle,
        forward,
    )

    convolved = pl.pallas_call(
        functools.partial(convolve_kernel, count),
        out_shape=jax.ShapeDtypeStruct((blocks, channels, span), BF16),
        scratch_shapes=[
            pltpu.VMEM((blocks * channels, span), F32),
            pltpu.VMEM((blocks * channels, span), F32),
        ],
        name="convolve",
    )(arrived, spec, first, last, twiddle, forward, backward)

    returned = lax.all_to_all(convolved, "seq", split_axis=0, concat_axis=0, tiled=True)
    mixed = pl.pallas_call(
        mix_kernel,
        grid=(width // chunk,),
        in_specs=[
            swapped,
            natural,
            natural,
            natural,
            pl.BlockSpec((1, chunk), lambda i: (0, i)),
        ],
        out_specs=natural,
        out_shape=jax.ShapeDtypeStruct((span, width), BF16),
        name="mix",
    )(returned.reshape(width, span), signal, gate_in, gate_out, skip_gain[None])
    return mixed[None]


def solution(mesh):
    row = P("grp", "seq", None)
    return jax.shard_map(
        per_device,
        mesh=mesh,
        in_specs=(row, row, row) + (P(),) * 8,
        out_specs=row,
        check_vma=False,
    )
```

time: 362 us -> 83.4 us (0.23); the launches traced: 357 us -> 83 us
  waiting for transfers between devices: 136 us -> 0.01 us
  local copies, waits for them, and re-layouts: 54.5 us -> 5.8 us
  blocking collectives: 80 us -> 32.2 us
  starting transfers between devices: 48.6 us -> 14.2 us
  Pallas kernels: 0 us -> 30.7 us
  matrix products: 20.3 us -> 0 us
  other arithmetic: 17.2 us -> 0.01 us
    all_to_all x7 -> x1, waiting for transfers between devices: 136 us -> 0.01 us  [per_device(): lax.all_to_all(gated.reshape(blocks, channels, span), 'seq', split_axis=0...]
    all_to_all x2 -> x1, blocking collectives: 80 us -> 32.2 us  [per_device(): lax.all_to_all(convolved, 'seq', split_axis=0, concat_axis=0, tiled=True)]
    all_to_all x7 -> x1, starting transfers between devices: 48.6 us -> 14.2 us  [per_device(): lax.all_to_all(gated.reshape(blocks, channels, span), 'seq', split_axis=0...]
    pallas_call x0 -> x4, Pallas kernels: none -> 30.7 us  [the longest x1 15.6 us: per_device(): pl.pallas_call(functools.partial(filter_kernel, length, count), out_shape...]
    all_to_all x12 -> x0, local copies, waits for them, and re-layouts: 22.7 us -> none  [the longest x2 8.94 us: in_one_piece(): lax.all_to_all(both, axis, split_axis=split_dim, concat_axis=concat_dim,...]
    dot_general x16 -> x0, matrix products: 20.3 us -> none  [the longest x2 5.32 us: forward_rows(): jnp.einsum('rkb,rbc->rkc', forward_stack, part_imag, preferred_element_ty...]
    unnamed x27 -> x17, local copies, waits for them, and re-layouts: 12.9 us -> 3.57 us
    reshape x4 -> x0, local copies, waits for them, and re-layouts: 8.49 us -> none  [the longest x2 4.26 us: first_section(): imag_part.reshape(rows_freq, per_block, channels)]
  transfers between devices with their start and end apart: 7 -> 1, of which waited for: 6 -> 0; matrix products, arithmetic and copies ran while one was open for 14% -> 5% of each run, Pallas kernels for 0% -> 19%
where the time goes in v1:
time: 83.4 us; the launch traced here: 83 us
  blocking collectives  32.2 us (39%)
  Pallas kernels  30.7 us (37%)
  starting transfers between devices  14.2 us (17%)
  local copies, waits for them, and re-layouts  5.8 us (7%)
    all_to_all x1, blocking collectives, per_device(): lax.all_to_all(convolved, 'seq', split_axis=0, concat_axis=0, tiled=True)  32.2 us
    pallas_call x1, Pallas kernels, per_device(): pl.pallas_call(functools.partial(filter_kernel, length, count), out_shape...  15.6 us
    all_to_all x1, starting transfers between devices, per_device(): lax.all_to_all(gated.reshape(blocks, channels, span), 'seq', split_axis=0...  14.2 us
    pallas_call x1, Pallas kernels, per_device(): pl.pallas_call(functools.partial(convolve_kernel, count), out_shape=jax.S...  7.84 us
    pallas_call x1, Pallas kernels, per_device(): pl.pallas_call(mix_kernel, grid=(width // chunk,), in_specs=[swapped, nat...  3.7 us
    unnamed x17, local copies, waits for them, and re-layouts  3.57 us
    pallas_call x1, Pallas kernels, per_device(): pl.pallas_call(gate_kernel, grid=(width // chunk,), in_specs=[natural, na...  3.52 us
  transfers between devices with their start and end apart: 1, of which 0 were waited for; matrix products, arithmetic and copies ran while one was open for 5% of the time, Pallas kernels for 19%

profile of v1, /device:TPU:32, one launch (start us, length us, event | category | flops | bytes accessed | tf_op | source)
XLA Modules:
  0.0 83.0 jit_solution(13796353662654412515)
XLA Ops:
  0.0 0.0 copy-start
  0.0 3.5 %gate.1 = bf16[2048,128]{1,0:T(8,128)(2,1)} custom-call(bf16[128,2048]{1,0:T(8,128)(2,1)} %bitcast.15, bf16[128,2048]{1,0:T(8,128)(2,1)} %bitcast.17), custom_call_target="tpu_custom_call" | custom-call | tf_op jit(solution)/shard_map/gate/pallas_call | solution.py:254
  3.5 14.2 %all-to-all-start = ((bf16[64,32,128]{2,1,0:T(8,128)(2,1)}), bf16[64,32,128]{2,1,0:T(8,128)(2,1)S(1)}, u32[]{:S(2)}, u32[]{:S(2)}) async-start(bf16[64,32,128]{2,1,0:T(8,128)(2,1)} %bitcast.19), calls=%async_computation | async-start | bytes 1048576 | tf_op jit(solution)/shard_map/all_to_all | solution.py:263
  17.8 0.0 copy-start.6
  17.8 0.8 dynamic-slice_bitcast_fusion
  18.5 0.7 copy.28.decay_ref
  19.2 0.0 copy-start.4
  19.2 0.0 copy-start.5
  19.2 0.0 copy-done.6
  19.2 0.7 copy-done.4
  19.9 0.0 copy-done.5
  19.9 0.7 copy.25
  20.6 0.0 copy-done
  20.6 0.0 copy-start.3
  20.6 0.1 constant_dynamic-slice_fusion
  20.7 0.0 copy-start.2
  20.7 0.7 copy.29
  21.4 0.0 copy-done.3
  21.4 0.7 copy.24
  22.1 0.0 copy-done.2
  22.1 0.7 copy.26
  22.8 15.6 %filter.1.spec_ref = bf16[8,256,256]{2,1,0:T(8,128)(2,1)} custom-call(f32[64,33]{1,0:T(8,128)} %bitcast.24, f32[64,4]{1,0:T(8,128)} %bitcast.23, f32[2,64,64]{2,1,0:T(8,128)} %bitcast.22, f32[32,64]{1,0:T(8,128)} %bitcast.25, f32[32,1]{1,0:T(8,128)} %copy.28.decay_ref, bf16[128,64]{1,0:T(8,128)(2,1)} %constant.20.clone.first_ref, ...), custom_call_target="tpu_custom_call" | custom-call | flops 20000000000 | bytes 2000000 | tf_op jit(solution)/shard_map/filter/pallas_call | solution.py:270
  38.4 0.0 all-to-all-done.data_ref
  38.4 0.0 copy-start.1
  38.4 0.8 copy-done.1
  39.2 7.8 %convolve.1 = bf16[64,32,128]{2,1,0:T(8,128)(2,1)} custom-call(bf16[64,32,128]{2,1,0:T(8,128)(2,1)} %copy-done.1, bf16[8,256,256]{2,1,0:T(8,128)(2,1)} %filter.1.spec_ref, bf16[128,64]{1,0:T(8,128)(2,1)} %constant.20.clone.first_ref, bf16[64,128]{1,0:T(8,128)(2,1)} %constant.21.clone.last_ref, f32[2,64,128]{2,1,0:T(8,128)} %constant.22.clone.twiddle_ref, ...), custom_call_target="tpu_custom_call" | custom-call | tf_op jit(solution)/shard_map/convolve/pallas_call | solution.py:292
  47.1 32.2 %all_to_all.10 = bf16[64,32,128]{2,1,0:T(8,128)(2,1)} all-to-all(bf16[64,32,128]{2,1,0:T(8,128)(2,1)} %convolve.1), channel_id=1, replica_groups=mesh['grp'=4,'seq'=64] {'seq'}, dimensions={0} | all-to-all | bytes 1048576 | tf_op jit(solution)/shard_map/all_to_all | solution.py:302
  79.2 3.7 %mix.1 = bf16[128,2048]{1,0:T(8,128)(2,1)} custom-call(bf16[2048,128]{1,0:T(8,128)(2,1)} %bitcast.20, bf16[128,2048]{1,0:T(8,128)(2,1)} %bitcast.16, bf16[128,2048]{1,0:T(8,128)(2,1)} %bitcast.18, bf16[128,2048]{1,0:T(8,128)(2,1)} %bitcast.21, f32[1,2048]{1,0:T(1,128)} %bitcast.26), custom_call_target="tpu_custom_call" | custom-call | tf_op jit(solution)/shard_map/mix/pallas_call | solution.py:303
  (1 shorter events, 0.0 us)
Async XLA Ops:
  0.0 20.6 %copy-start = (f32[64,2048]{1,0:T(8,128)S(1)}, f32[64,2048]{1,0:T(8,128)}, u32[]{:S(2)}) copy-start(f32[64,2048]{1,0:T(8,128)} %param.24) | copy-start | bytes 1572868
  3.5 34.9 %all-to-all-start = ((bf16[64,32,128]{2,1,0:T(8,128)(2,1)}), bf16[64,32,128]{2,1,0:T(8,128)(2,1)S(1)}, u32[]{:S(2)}, u32[]{:S(2)}) async-start(bf16[64,32,128]{2,1,0:T(8,128)(2,1)} %bitcast.19), calls=%async_computation | async-start | bytes 1048576 | tf_op jit(solution)/shard_map/all_to_all | solution.py:263
  17.8 1.5 %copy-start.6 = (f32[64]{0:T(128)S(1)}, f32[64]{0:T(128)}, u32[]{:S(2)}) copy-start(f32[64]{0:T(128)} %param.23) | copy-start | bytes 772
  19.2 0.7 copy-start.4
  19.2 0.7 copy-start.5
  20.6 0.8 copy-start.3
  20.7 1.4 %copy-start.2 = (f32[2,64,64]{2,1,0:T(8,128)S(1)}, f32[2,64,64]{2,1,0:T(8,128)}, u32[]{:S(2)}) copy-start(f32[2,64,64]{2,1,0:T(8,128)} %param.21) | copy-start | bytes 98308
  38.4 0.8 copy-start.1

commit v2 on v1

--- a/solution.py
+++ b/solution.py
@@ -10,9 +10,11 @@
 
 FLOOR_SHIFT = 0.05
 EPSILON = 1e-06
-HIGHEST = lax.Precision.HIGHEST
 F32 = jnp.float32
 BF16 = jnp.bfloat16
+STEP_BLOCKS = 4
+UNROLL_POSITIONS = 2
+UNROLL_GROUPS = 2
 SINE = (
     6.283182818534707,
     -41.34142139736154,
@@ -52,9 +54,36 @@
     )
 
 
-def gate_kernel(signal_ref, gate_ref, out_ref):
-    gated = gate_ref[...].astype(F32) * signal_ref[...].astype(F32)
-    out_ref[...] = gated.astype(BF16).T
+def column_copies(sources, places, sems, chunk):
+    width = sources[0].shape[1]
+    return [
+        [
+            pltpu.make_async_copy(
+                source.at[:, pl.ds(k * chunk, chunk)],
+                place.at[:, pl.ds(k * chunk, chunk)],
+                sems.at[i, k],
+            )
+            for i, (source, place) in enumerate(zip(sources, places))
+        ]
+        for k in range(width // chunk)
+    ]
+
+
+def gate_kernel(chunk, signal_hbm, gate_hbm, out_hbm, signal_ref, gate_ref, out_ref, sems, out_sems):
+    copies = column_copies((signal_hbm, gate_hbm), (signal_ref, gate_ref), sems, chunk)
+    for copy in sum(copies, []):
+        copy.start()
+    sent = []
+    for k, pair in enumerate(copies):
+        for copy in pair:
+            copy.wait()
+        at = pl.ds(k * chunk, chunk)
+        gated = gate_ref[:, at].astype(F32) * signal_ref[:, at].astype(F32)
+        out_ref[at, :] = gated.astype(BF16).T
+        sent.append(pltpu.make_async_copy(out_ref.at[at, :], out_hbm.at[at, :], out_sems.at[k]))
+        sent[-1].start()
+    for copy in sent:
+        copy.wait()
 
 
 def spectrum_of(rows_ref, group, count, blocks, channels, first, twiddle_ref, forward):
@@ -81,34 +110,84 @@
     return jnp.dot(jnp.concatenate(turned, axis=0), forward, preferred_element_type=F32)
 
 
+def split_three(value):
+    high = value.astype(BF16)
+    rest = value - high.astype(F32)
+    middle = rest.astype(BF16)
+    low = (rest - middle.astype(F32)).astype(BF16)
+    return high, middle, low
+
+
+def split_weights(weight):
+    high, middle, low = split_three(weight)
+    return jnp.concatenate([high, middle, low, high, middle, high], axis=1)
+
+
+def dot_split(weights, value):
+    high, middle, low = split_three(value)
+    stacked = jnp.concatenate([high, high, high, middle, middle, low], axis=0)
+    return jnp.dot(weights, stacked, preferred_element_type=F32)
+
+
 def filter_kernel(
     total,
     count,
+    step_blocks,
     pos_weight_ref,
-    columns_ref,
+    pos_bias_ref,
     inner_ref,
-    out_weight_ref,
-    decay_ref,
+    inner_bias_ref,
+    frequency_ref,
+    out_weight_hbm,
+    decay_hbm,
     first_ref,
     twiddle_ref,
     forward_ref,
     spec_ref,
     taps_ref,
     square_ref,
+    own_ref,
+    turned_ref,
+    sems,
 ):
-    channels = out_weight_ref.shape[0]
     span = taps_ref.shape[1]
+    channels = square_ref.shape[0]
     blocks = taps_ref.shape[0] // channels
-    step_blocks = 8
     width = step_blocks * span
-    layers = inner_ref.shape[0]
-    bands = (pos_weight_ref.shape[1] - 1) // 2
-    frequency = columns_ref[:, 0:1]
-    turns_per = frequency * (1.0 / (2.0 * np.pi))
-    biases = [columns_ref[:, i + 1 : i + 2] for i in range(layers + 1)]
-    weight_time = pos_weight_ref[:, 0:1]
-    weight_tone = pos_weight_ref[:, 1:]
-    decay = decay_ref[...]
+    layers, order = inner_bias_ref.shape
+    bands = (pos_weight_ref.shape[0] - 1) // 2
+    lanes = own_ref.shape[1]
+    start = lax.axis_index("seq") * channels
+    inside = pl.multiple_of(start % lanes, channels)
+    outside = pl.multiple_of((start // lanes) * lanes, lanes)
+    copies = [
+        pltpu.make_async_copy(
+            out_weight_hbm.at[:, pl.ds(outside, lanes)], own_ref.at[pl.ds(0, order), :], sems.at[0]
+        ),
+        pltpu.make_async_copy(
+            decay_hbm.at[:, pl.ds(outside, lanes)], own_ref.at[pl.ds(order, 1), :], sems.at[1]
+        ),
+    ]
+    own_ref[pl.ds(order, own_ref.shape[0] - order), :] = jnp.zeros(
+        (own_ref.shape[0] - order, lanes), F32
+    )
+    for copy in copies:
+        copy.start()
+    turns_per = frequency_ref[...] * (1.0 / (2.0 * np.pi))
+    rows = [turns_per * pos_bias_ref[...], turns_per * pos_weight_ref[0:1, :]]
+    rows += [turns_per * inner_bias_ref[i : i + 1, :] for i in range(layers)]
+    rows.append(jnp.zeros((8 - len(rows), order), F32))
+    columns = jnp.concatenate(rows, axis=0).T
+    bias, time_weight = columns[:, 0:1], columns[:, 1:2]
+    biases = [columns[:, i + 2 : i + 3] for i in range(layers)]
+    tone_weight = split_weights((pos_weight_ref[1:, :] * turns_per).T)
+    inner = [split_weights((inner_ref[i] * turns_per).T) for i in range(layers)]
+    for copy in copies:
+        copy.wait()
+    turned_ref[...] = own_ref[...].T
+    own = turned_ref[pl.ds(inside, channels), :]
+    out_weight = split_weights(own[:, :order])
+    decay = own[:, order : order + 1]
     tone = 0.0001 + lax.broadcasted_iota(jnp.int32, (bands, 1), 0).astype(F32) * (
         (bands - 1 - 0.0001) / (bands - 1)
     )
@@ -123,15 +202,10 @@
         features = jnp.concatenate(
             [sine_of_turns(angle + 0.25), -sine_of_turns(angle)], axis=0
         )
-        pre = jnp.dot(weight_tone, features, precision=HIGHEST, preferred_element_type=F32)
-        hidden = sine_of_turns(turns_per * (pre + weight_time * moment + biases[0]))
+        hidden = sine_of_turns(dot_split(tone_weight, features) + (time_weight * moment + bias))
         for i in range(layers):
-            pre = jnp.dot(inner_ref[i], hidden, precision=HIGHEST, preferred_element_type=F32)
-            hidden = sine_of_turns(turns_per * (pre + biases[i + 1]))
-        shaped = jnp.dot(
-            out_weight_ref[...], hidden, precision=HIGHEST, preferred_element_type=F32
-        )
-        raw = shaped * (jnp.exp(-moment * decay) + FLOOR_SHIFT)
+            hidden = sine_of_turns(dot_split(inner[i], hidden) + biases[i])
+        raw = dot_split(out_weight, hidden) * (jnp.exp(-moment * decay) + FLOOR_SHIFT)
         squares = raw * raw
         folded = square_ref[...]
         for j in range(step_blocks):
@@ -141,7 +215,7 @@
         square_ref[...] = folded
         return carry
 
-    lax.fori_loop(0, blocks // step_blocks, positions_step, 0)
+    lax.fori_loop(0, blocks // step_blocks, positions_step, 0, unroll=UNROLL_POSITIONS)
     summed = jnp.sum(square_ref[...], axis=1, keepdims=True)
     square_ref[...] = jnp.broadcast_to(lax.rsqrt(summed + EPSILON), square_ref.shape)
 
@@ -157,7 +231,7 @@
         spec_ref[group] = jnp.concatenate(pieces, axis=0)
         return carry
 
-    lax.fori_loop(0, channels // count, spectrum_step, 0)
+    lax.fori_loop(0, channels // count, spectrum_step, 0, unroll=UNROLL_GROUPS)
 
 
 def convolve_kernel(
@@ -214,15 +288,28 @@
             ]
         return carry
 
-    lax.fori_loop(0, channels // count, group_step, 0)
+    lax.fori_loop(0, channels // count, group_step, 0, unroll=UNROLL_GROUPS)
     out_ref[...] = result_ref[...].reshape(blocks, channels, span).astype(BF16)
 
 
-def mix_kernel(conv_ref, signal_ref, gate_in_ref, gate_out_ref, skip_ref, out_ref):
-    gated = (gate_in_ref[...].astype(F32) * signal_ref[...].astype(F32)).astype(BF16)
-    conv = conv_ref[...].T.astype(F32)
-    mixed = gate_out_ref[...].astype(F32) * (conv + skip_ref[...] * gated.astype(F32))
-    out_ref[...] = mixed.astype(BF16)
+def stage_kernel(signal_ref, gate_ref, out_gate_ref, skip_ref, direct_ref, held_ref):
+    gated = (gate_ref[...].astype(F32) * signal_ref[...].astype(F32)).astype(BF16)
+    direct_ref[...] = skip_ref[...] * gated.astype(F32)
+    held_ref[...] = out_gate_ref[...]
+
+
+def mix_kernel(chunk, conv_ref, direct_ref, held_ref, out_hbm, out_ref, sems):
+    width = direct_ref.shape[1]
+    copies = []
+    for k in range(width // chunk):
+        at = pl.ds(k * chunk, chunk)
+        conv = conv_ref[at, :].T.astype(F32)
+        mixed = held_ref[:, at].astype(F32) * (conv + direct_ref[:, at])
+        out_ref[:, at] = mixed.astype(BF16)
+        copies.append(pltpu.make_async_copy(out_ref.at[:, at], out_hbm.at[:, at], sems.at[k]))
+        copies[-1].start()
+    for copy in copies:
+        copy.wait()
 
 
 def per_device(
@@ -239,24 +326,35 @@
     skip_gain,
 ):
     blocks = lax.axis_size("seq")
-    block_id = lax.axis_index("seq")
     span, width = signal.shape[1:]
     channels = width // blocks
+    order = out_weight.shape[0]
     length = blocks * span
     signal, gate_in, gate_out = signal[0], gate_in[0], gate_out[0]
     first, last, twiddle, forward, backward = transform_tables(blocks, span)
     chunk = 512
+    chunks = width // chunk
     count = 4
     groups = channels // count
-
-    natural = pl.BlockSpec((span, chunk), lambda i: (0, i))
-    swapped = pl.BlockSpec((chunk, span), lambda i: (i, 0))
+    vmem = pl.BlockSpec(memory_space=pltpu.VMEM)
+    hbm = pl.BlockSpec(memory_space=pltpu.HBM)
+
+    def params(mebibytes):
+        return pltpu.CompilerParams(vmem_limit_bytes=mebibytes * 2**20)
+
     gated = pl.pallas_call(
-        gate_kernel,
-        grid=(width // chunk,),
-        in_specs=[natural, natural],
-        out_specs=swapped,
+        functools.partial(gate_kernel, chunk),
+        in_specs=[hbm, hbm],
+        out_specs=hbm,
         out_shape=jax.ShapeDtypeStruct((width, span), BF16),
+        scratch_shapes=[
+            pltpu.VMEM((span, width), BF16),
+            pltpu.VMEM((span, width), BF16),
+            pltpu.VMEM((width, span), BF16),
+            pltpu.SemaphoreType.DMA((2, chunks)),
+            pltpu.SemaphoreType.DMA((chunks,)),
+        ],
+        compiler_params=params(60),
         name="gate",
     )(signal, gate_in)
 
@@ -264,26 +362,32 @@
         gated.reshape(blocks, channels, span), "seq", split_axis=0, concat_axis=0, tiled=True
     )
 
-    own_weight = lax.dynamic_slice_in_dim(out_weight, block_id * channels, channels, axis=1).T
-    own_decay = lax.dynamic_slice_in_dim(decay_rates, block_id * channels, channels, axis=0)[:, None]
-    columns = jnp.concatenate([frequency[None], pos_bias[None], inner_bias], axis=0).T
+    lanes = span
     spec = pl.pallas_call(
-        functools.partial(filter_kernel, length, count),
-        out_shape=jax.ShapeDtypeStruct((groups, count * blocks, 2 * span), BF16),
+        functools.partial(filter_kernel, length, count, STEP_BLOCKS),
+        in_specs=[vmem] * 5 + [hbm, hbm] + [vmem] * 3,
+        out_specs=vmem,
+        out_shape=pltpu.VMEM((groups, count * blocks, 2 * span), BF16),
         scratch_shapes=[
             pltpu.VMEM((blocks * channels, span), F32),
             pltpu.VMEM((channels, span), F32),
+            pltpu.VMEM((2 * blocks, lanes), F32),
+            pltpu.VMEM((lanes, 2 * blocks), F32),
+            pltpu.SemaphoreType.DMA((2,)),
         ],
         cost_estimate=pl.CostEstimate(
             flops=20_000_000_000, bytes_accessed=2_000_000, transcendentals=2_000_000
         ),
+        compiler_params=params(12),
         name="filter",
     )(
-        pos_weight.T,
-        columns,
-        jnp.swapaxes(inner_weight, 1, 2),
-        own_weight,
-        own_decay,
+        pos_weight,
+        pos_bias[None],
+        inner_weight,
+        inner_bias,
+        frequency[None],
+        out_weight,
+        decay_rates[None],
         first,
         twiddle,
         forward,
@@ -291,29 +395,43 @@
 
     convolved = pl.pallas_call(
         functools.partial(convolve_kernel, count),
-        out_shape=jax.ShapeDtypeStruct((blocks, channels, span), BF16),
+        in_specs=[vmem] * 7,
+        out_specs=vmem,
+        out_shape=pltpu.VMEM((blocks, channels, span), BF16),
         scratch_shapes=[
             pltpu.VMEM((blocks * channels, span), F32),
             pltpu.VMEM((blocks * channels, span), F32),
         ],
+        compiler_params=params(12),
         name="convolve",
     )(arrived, spec, first, last, twiddle, forward, backward)
 
     returned = lax.all_to_all(convolved, "seq", split_axis=0, concat_axis=0, tiled=True)
+
+    signal, gate_in, gate_out, _ = lax.optimization_barrier(
+        (signal, gate_in, gate_out, convolved)
+    )
+    direct, held = pl.pallas_call(
+        stage_kernel,
+        in_specs=[vmem] * 4,
+        out_specs=[vmem, vmem],
+        out_shape=[pltpu.VMEM((span, width), F32), pltpu.VMEM((span, width), BF16)],
+        cost_estimate=pl.CostEstimate(
+            flops=10_000_000_000, bytes_accessed=2_000_000, transcendentals=0
+        ),
+        compiler_params=params(8),
+        name="stage",
+    )(signal, gate_in, gate_out, skip_gain[None])
+
     mixed = pl.pallas_call(
-        mix_kernel,
-        grid=(width // chunk,),
-        in_specs=[
-            swapped,
-            natural,
-            natural,
-            natural,
-            pl.BlockSpec((1, chunk), lambda i: (0, i)),
-        ],
-        out_specs=natural,
+        functools.partial(mix_kernel, chunk),
+        in_specs=[vmem] * 3,
+        out_specs=hbm,
         out_shape=jax.ShapeDtypeStruct((span, width), BF16),
+        scratch_shapes=[pltpu.VMEM((span, width), BF16), pltpu.SemaphoreType.DMA((chunks,))],
+        compiler_params=params(8),
         name="mix",
-    )(returned.reshape(width, span), signal, gate_in, gate_out, skip_gain[None])
+    )(returned.reshape(width, span), direct, held)
     return mixed[None]
 
 

time: 83.4 us -> 72.8 us (0.87)
  blocking collectives: 32.2 us -> 0 us
  waiting for transfers between devices: 0.01 us -> 20.8 us
  starting transfers between devices: 14.2 us -> 24.6 us
  Pallas kernels: 30.7 us -> 25.3 us
  local copies, waits for them, and re-layouts: 5.8 us -> 1.7 us
    all_to_all x1 -> x0, blocking collectives: 32.2 us -> none  [per_device(): lax.all_to_all(convolved, 'seq', split_axis=0, concat_axis=0, tiled=True)]
    all_to_all x0 -> x1, waiting for transfers between devices: none -> 18 us  [per_device(): lax.all_to_all(convolved, 'seq', split_axis=0, concat_axis=0, tiled=True)]
    all_to_all x0 -> x1, starting transfers between devices: none -> 10.2 us  [per_device(): lax.all_to_all(convolved, 'seq', split_axis=0, concat_axis=0, tiled=True)]
    pallas_call x4 -> x5, Pallas kernels: 30.7 us -> 25.3 us  [the longest x1 16.5 us: per_device(): pl.pallas_call(functools.partial(filter_kernel, length, count, STEP_BLOCK...]
    all_to_all x1, waiting for transfers between devices: 0.01 us -> 2.72 us  [per_device(): lax.all_to_all(gated.reshape(blocks, channels, span), 'seq', split_axis=0...]
    unnamed x17 -> x32, local copies, waits for them, and re-layouts: 3.57 us -> 1.7 us
    broadcast_in_dim x2 -> x0, local copies, waits for them, and re-layouts: 1.45 us -> none  [per_device(): lax.dynamic_slice_in_dim(decay_rates, block_id * channels, channels, axis=0)]
  transfers between devices with their start and end apart: 1 -> 2, of which waited for: 0 -> 2; matrix products, arithmetic and copies ran while one was open for 5% -> 0% of each run, Pallas kernels for 19% -> 23%
where the time goes in v2:
time: 72.8 us; the launch traced here: 72.5 us
  Pallas kernels  25.3 us (35%)
  starting transfers between devices  24.6 us (34%)
  waiting for transfers between devices  20.8 us (29%)
  local copies, waits for them, and re-layouts  1.7 us (2%)
    all_to_all x1, waiting for transfers between devices, per_device(): lax.all_to_all(convolved, 'seq', split_axis=0, concat_axis=0, tiled=True)  18 us
    pallas_call x1, Pallas kernels, per_device(): pl.pallas_call(functools.partial(filter_kernel, length, count, STEP_BLOCK...  16.5 us
    all_to_all x1, starting transfers between devices, per_device(): lax.all_to_all(gated.reshape(blocks, channels, span), 'seq', split_axis=0...  14.4 us
    all_to_all x1, starting transfers between devices, per_device(): lax.all_to_all(convolved, 'seq', split_axis=0, concat_axis=0, tiled=True)  10.2 us
    pallas_call x1, Pallas kernels, per_device(): pl.pallas_call(functools.partial(convolve_kernel, count), in_specs=[vmem]...  5.53 us
    all_to_all x1, waiting for transfers between devices, per_device(): lax.all_to_all(gated.reshape(blocks, channels, span), 'seq', split_axis=0...  2.72 us
    pallas_call x1, Pallas kernels, per_device(): pl.pallas_call(functools.partial(gate_kernel, chunk), in_specs=[hbm, hbm]...  2.15 us
    unnamed x32, local copies, waits for them, and re-layouts  1.7 us
  transfers between devices with their start and end apart: 2, of which 2 were waited for; matrix products, arithmetic and copies ran while one was open for 0% of the time, Pallas kernels for 23%

profile of v2, /device:TPU:32, one launch (start us, length us, event | category | flops | bytes accessed | tf_op | source)
XLA Modules:
  0.0 72.5 jit_solution(4580904448277196454)
XLA Ops:
  0.0 2.2 %gate.1 = bf16[2048,128]{1,0:T(8,128)(2,1)} custom-call(bf16[128,2048]{1,0:T(8,128)(2,1)} %bitcast.11, bf16[128,2048]{1,0:T(8,128)(2,1)} %bitcast.13), custom_call_target="tpu_custom_call" | custom-call | tf_op jit(solution)/shard_map/gate/pallas_call | solution.py:345
  2.2 0.0 copy-start.2
  2.2 0.0 copy-start.4
  2.2 0.0 copy-start.5
  2.2 0.0 copy-start.7
  2.2 0.0 copy-start.9
  2.2 0.0 copy-start.10
  2.2 0.0 copy-start.11
  2.2 0.0 copy-start.15
  2.3 14.4 %all-to-all-start = ((bf16[64,32,128]{2,1,0:T(8,128)(2,1)}), bf16[64,32,128]{2,1,0:T(8,128)(2,1)S(1)}, u32[]{:S(2)}, u32[]{:S(2)}) async-start(bf16[64,32,128]{2,1,0:T(8,128)(2,1)} %bitcast.20), calls=%async_computation | async-start | bytes 1048576 | tf_op jit(solution)/shard_map/all_to_all | solution.py:361
  16.6 0.0 copy-start.13
  16.6 0.0 copy-start.14
  16.7 0.0 copy-done.2
  16.7 0.0 copy-done.4
  16.7 0.0 copy-done.5
  16.7 0.0 copy-done.7
  16.7 0.0 copy-done.9
  16.7 0.0 copy-done.10
  16.7 0.0 copy-done.11
  16.7 0.6 copy-done.13
  17.3 16.5 %filter.1.spec_ref = bf16[8,256,256]{2,1,0:T(8,128)(2,1)S(1)} custom-call(f32[33,64]{1,0:T(8,128)S(1)} %copy-done.10, f32[1,64]{1,0:T(1,128)S(1)} %bitcast.18, f32[2,64,64]{2,1,0:T(8,128)S(1)} %copy-done.9, f32[2,64]{1,0:T(2,128)S(1)} %copy-done.13, f32[1,64]{1,0:T(1,128)S(1)} %bitcast.19, f32[64,2048]{1,0:T(8,128)S(1)} %copy-done.7, ...), custom_call_target="tpu_custom_call" | custom-call | flops 20000000000 | bytes 2000000 | tf_op jit(solution)/shard_map/filter/pallas_call | solution.py:366
  33.8 2.7 %all-to-all-done.data_ref = bf16[64,32,128]{2,1,0:T(8,128)(2,1)S(1)} async-done(((bf16[64,32,128]{2,1,0:T(8,128)(2,1)}), bf16[64,32,128]{2,1,0:T(8,128)(2,1)S(1)}, u32[]{:S(2)}, u32[]{:S(2)}) %all-to-all-start) | async-done | bytes 524320 | tf_op jit(solution)/shard_map/all_to_all | solution.py:361
  36.5 5.5 %convolve.1 = bf16[64,32,128]{2,1,0:T(8,128)(2,1)} custom-call(bf16[64,32,128]{2,1,0:T(8,128)(2,1)S(1)} %all-to-all-done.data_ref, bf16[8,256,256]{2,1,0:T(8,128)(2,1)S(1)} %filter.1.spec_ref, bf16[128,64]{1,0:T(8,128)(2,1)S(1)} %copy-done.5, bf16[64,128]{1,0:T(8,128)(2,1)S(1)} %copy-done.6, f32[2,64,128]{2,1,0:T(8,128)S(1)} %copy-done.4, ...), custom_call_target="tpu_custom_call" | custom-call | tf_op jit(solution)/shard_map/convolve/pallas_call | solution.py:396
  42.1 10.2 %all-to-all-start.1 = ((bf16[64,32,128]{2,1,0:T(8,128)(2,1)}), bf16[64,32,128]{2,1,0:T(8,128)(2,1)S(1)}, u32[]{:S(2)}, u32[]{:S(2)}) async-start(bf16[64,32,128]{2,1,0:T(8,128)(2,1)} %convolve.1), calls=%async_computation.1 | async-start | bytes 1048576 | tf_op jit(solution)/shard_map/all_to_all | solution.py:409
  52.3 0.0 copy-done.12
  52.3 0.0 copy-done
  52.3 0.0 copy-done.1
  52.3 0.0 copy-start.8
  52.3 1.0 %copy-done.8 = bf16[1,128,2048]{2,1,0:T(8,128)(2,1)S(1)} copy-done((bf16[1,128,2048]{2,1,0:T(8,128)(2,1)S(1)}, bf16[1,128,2048]{2,1,0:T(8,128)(2,1)}, u32[]{:S(2)}) %copy-start.8) | copy-done | bytes 524312
  53.3 0.2 stage.1
  53.5 18.0 %all-to-all-done.1 = bf16[64,32,128]{2,1,0:T(8,128)(2,1)S(1)} async-done(((bf16[64,32,128]{2,1,0:T(8,128)(2,1)}), bf16[64,32,128]{2,1,0:T(8,128)(2,1)S(1)}, u32[]{:S(2)}, u32[]{:S(2)}) %all-to-all-start.1) | async-done | bytes 524320 | tf_op jit(solution)/shard_map/all_to_all | solution.py:409
  71.6 0.9 %mix.1 = bf16[128,2048]{1,0:T(8,128)(2,1)} custom-call(bf16[2048,128]{1,0:T(8,128)(2,1)S(1)} %bitcast.10, f32[128,2048]{1,0:T(8,128)S(1)} %get-tuple-element.13.direct_ref, bf16[128,2048]{1,0:T(8,128)(2,1)S(1)} %get-tuple-element.14.held_ref), custom_call_target="tpu_custom_call" | custom-call | tf_op jit(solution)/shard_map/mix/pallas_call | solution.py:426
  (9 shorter events, 0.0 us)
Async XLA Ops:
  2.2 14.5 %copy-start.2 = (bf16[256,256]{1,0:T(8,128)(2,1)S(1)}, bf16[256,256]{1,0:T(8,128)(2,1)}, u32[]{:S(2)}) copy-start(bf16[256,256]{1,0:T(8,128)(2,1)} %constant.13.clone.forward_ref) | copy-start | bytes 393220
  2.2 14.5 %copy-start.4 = (f32[2,64,128]{2,1,0:T(8,128)S(1)}, f32[2,64,128]{2,1,0:T(8,128)}, u32[]{:S(2)}) copy-start(f32[2,64,128]{2,1,0:T(8,128)} %constant.12.clone.twiddle_ref) | copy-start | bytes 196612
  2.2 14.5 %copy-start.5 = (bf16[128,64]{1,0:T(8,128)(2,1)S(1)}, bf16[128,64]{1,0:T(8,128)(2,1)}, u32[]{:S(2)}) copy-start(bf16[128,64]{1,0:T(8,128)(2,1)} %constant.10.clone.first_ref) | copy-start | bytes 49156
  2.2 14.5 %copy-start.7 = (f32[64,2048]{1,0:T(8,128)S(1)}, f32[64,2048]{1,0:T(8,128)}, u32[]{:S(2)}) copy-start(f32[64,2048]{1,0:T(8,128)} %out_weight_hbm.1) | copy-start | bytes 1572868
  2.2 14.5 %copy-start.9 = (f32[2,64,64]{2,1,0:T(8,128)S(1)}, f32[2,64,64]{2,1,0:T(8,128)}, u32[]{:S(2)}) copy-start(f32[2,64,64]{2,1,0:T(8,128)} %inner_ref.1) | copy-start | bytes 98308
  2.2 14.5 %copy-start.10 = (f32[33,64]{1,0:T(8,128)S(1)}, f32[33,64]{1,0:T(8,128)}, u32[]{:S(2)}) copy-start(f32[33,64]{1,0:T(8,128)} %pos_weight_ref.1) | copy-start | bytes 25348
  2.2 14.5 %copy-start.11 = (f32[2048]{0:T(1024)S(1)}, f32[2048]{0:T(1024)}, u32[]{:S(2)}) copy-start(f32[2048]{0:T(1024)} %param.25) | copy-start | bytes 24580
  2.2 14.5 %copy-start.15 = (f32[64]{0:T(128)S(1)}, f32[64]{0:T(128)}, u32[]{:S(2)}) copy-start(f32[64]{0:T(128)} %param.23) | copy-start | bytes 772
  2.3 34.3 %all-to-all-start = ((bf16[64,32,128]{2,1,0:T(8,128)(2,1)}), bf16[64,32,128]{2,1,0:T(8,128)(2,1)S(1)}, u32[]{:S(2)}, u32[]{:S(2)}) async-start(bf16[64,32,128]{2,1,0:T(8,128)(2,1)} %bitcast.20), calls=%async_computation | async-start | bytes 1048576 | tf_op jit(solution)/shard_map/all_to_all | solution.py:361
  16.6 0.7 copy-start.13
  16.6 0.7 copy-start.14
  17.3 19.2 %copy-start.3 = (bf16[256,256]{1,0:T(8,128)(2,1)S(1)}, bf16[256,256]{1,0:T(8,128)(2,1)}, u32[]{:S(2)}) copy-start(bf16[256,256]{1,0:T(8,128)(2,1)} %constant.14.clone.backward_ref) | copy-start | bytes 393220
  17.3 19.2 %copy-start.6 = (bf16[64,128]{1,0:T(8,128)(2,1)S(1)}, bf16[64,128]{1,0:T(8,128)(2,1)}, u32[]{:S(2)}) copy-start(bf16[64,128]{1,0:T(8,128)(2,1)} %constant.11.clone.last_ref) | copy-start | bytes 49156
  36.5 15.7 %copy-start.12 = (f32[2048]{0:T(1024)S(1)}, f32[2048]{0:T(1024)}, u32[]{:S(2)}) copy-start(f32[2048]{0:T(1024)} %param.26) | copy-start | bytes 24580
  42.0 10.2 %copy-start = (bf16[1,128,2048]{2,1,0:T(8,128)(2,1)S(1)}, bf16[1,128,2048]{2,1,0:T(8,128)(2,1)}, u32[]{:S(2)}) copy-start(bf16[1,128,2048]{2,1,0:T(8,128)(2,1)} %param.16) | copy-start | bytes 1572868
  42.1 10.2 %copy-start.1 = (bf16[1,128,2048]{2,1,0:T(8,128)(2,1)S(1)}, bf16[1,128,2048]{2,1,0:T(8,128)(2,1)}, u32[]{:S(2)}) copy-start(bf16[1,128,2048]{2,1,0:T(8,128)(2,1)} %param.17) | copy-start | bytes 1572868
  42.1 29.5 %all-to-all-start.1 = ((bf16[64,32,128]{2,1,0:T(8,128)(2,1)}), bf16[64,32,128]{2,1,0:T(8,128)(2,1)S(1)}, u32[]{:S(2)}, u32[]{:S(2)}) async-start(bf16[64,32,128]{2,1,0:T(8,128)(2,1)} %convolve.1), calls=%async_computation.1 | async-start | bytes 1048576 | tf_op jit(solution)/shard_map/all_to_all | solution.py:409
  52.3 1.0 %copy-start.8 = (bf16[1,128,2048]{2,1,0:T(8,128)(2,1)S(1)}, bf16[1,128,2048]{2,1,0:T(8,128)(2,1)}, u32[]{:S(2)}) copy-start(bf16[1,128,2048]{2,1,0:T(8,128)(2,1)} %param.18) | copy-start | bytes 1572868

commit v3 on v2

--- a/solution.py
+++ b/solution.py
@@ -10,11 +10,13 @@
 
 FLOOR_SHIFT = 0.05
 EPSILON = 1e-06
+SEQ_SHAPE = (4, 2, 8)
+SHIFT = (2, 1, 4)
 F32 = jnp.float32
 BF16 = jnp.bfloat16
-STEP_BLOCKS = 4
-UNROLL_POSITIONS = 2
+STEP_BLOCKS = 16
 UNROLL_GROUPS = 2
+EARLY = 1
 SINE = (
     6.283182818534707,
     -41.34142139736154,
@@ -32,6 +34,20 @@
     for factor in SINE[-2::-1]:
         poly = poly * r2 + factor
     return poly * r
+
+
+def exchange_order(shape):
+    at = np.indices(shape).reshape(len(shape), -1)
+    moved = [(place + by) % size for place, by, size in zip(at, SHIFT, shape)]
+    return np.ravel_multi_index(moved, shape)
+
+
+def place_in_order(index, shape):
+    place, stride = 0, 1
+    for by, size in zip(SHIFT[::-1], shape[::-1]):
+        place = place + stride * (((index // stride) % size + size - by) % size)
+        stride *= size
+    return place
 
 
 def transform_tables(blocks, span):
@@ -120,16 +136,25 @@
 
 def split_weights(weight):
     high, middle, low = split_three(weight)
-    return jnp.concatenate([high, middle, low, high, middle, high], axis=1)
+    none = jnp.zeros_like(high)
+    return jnp.concatenate(
+        [
+            jnp.concatenate([high, high, high], axis=1),
+            jnp.concatenate([middle, middle, none], axis=1),
+            jnp.concatenate([low, none, none], axis=1),
+        ],
+        axis=0,
+    )
 
 
 def dot_split(weights, value):
-    high, middle, low = split_three(value)
-    stacked = jnp.concatenate([high, high, high, middle, middle, low], axis=0)
-    return jnp.dot(weights, stacked, preferred_element_type=F32)
-
-
-def filter_kernel(
+    rows = weights.shape[0] // 3
+    stacked = jnp.concatenate(split_three(value), axis=0)
+    parts = jnp.dot(weights, stacked, preferred_element_type=F32)
+    return parts[:rows] + (parts[rows : 2 * rows] + parts[2 * rows :])
+
+
+def filter_body(
     total,
     count,
     step_blocks,
@@ -157,7 +182,7 @@
     layers, order = inner_bias_ref.shape
     bands = (pos_weight_ref.shape[0] - 1) // 2
     lanes = own_ref.shape[1]
-    start = lax.axis_index("seq") * channels
+    start = place_in_order(lax.axis_index("seq"), SEQ_SHAPE) * channels
     inside = pl.multiple_of(start % lanes, channels)
     outside = pl.multiple_of((start // lanes) * lanes, lanes)
     copies = [
@@ -215,7 +240,7 @@
         square_ref[...] = folded
         return carry
 
-    lax.fori_loop(0, blocks // step_blocks, positions_step, 0, unroll=UNROLL_POSITIONS)
+    lax.fori_loop(0, blocks // step_blocks, positions_step, 0)
     summed = jnp.sum(square_ref[...], axis=1, keepdims=True)
     square_ref[...] = jnp.broadcast_to(lax.rsqrt(summed + EPSILON), square_ref.shape)
 
@@ -232,6 +257,16 @@
         return carry
 
     lax.fori_loop(0, channels // count, spectrum_step, 0, unroll=UNROLL_GROUPS)
+
+
+def filter_kernel(turn, held, *args):
+    scalars, refs = args[:3], args[3:]
+    if held:
+        refs = refs[:10] + refs[11:]
+
+    @pl.when(lax.axis_index("grp") % 2 == turn)
+    def _():
+        filter_body(*scalars, *refs)
 
 
 def convolve_kernel(
@@ -328,13 +363,22 @@
     blocks = lax.axis_size("seq")
     span, width = signal.shape[1:]
     channels = width // blocks
-    order = out_weight.shape[0]
     length = blocks * span
     signal, gate_in, gate_out = signal[0], gate_in[0], gate_out[0]
     first, last, twiddle, forward, backward = transform_tables(blocks, span)
+    order = exchange_order(SEQ_SHAPE)
+    first_data, last = first[:, order], last[order]
+    exchange = functools.partial(
+        lax.all_to_all,
+        axis_name="seq",
+        split_axis=0,
+        concat_axis=0,
+        tiled=True,
+        axis_index_groups=[[int(i) for i in order]],
+    )
     chunk = 512
     chunks = width // chunk
-    count = 4
+    count = 16
     groups = channels // count
     vmem = pl.BlockSpec(memory_space=pltpu.VMEM)
     hbm = pl.BlockSpec(memory_space=pltpu.HBM)
@@ -358,40 +402,49 @@
         name="gate",
     )(signal, gate_in)
 
-    arrived = lax.all_to_all(
-        gated.reshape(blocks, channels, span), "seq", split_axis=0, concat_axis=0, tiled=True
-    )
-
     lanes = span
-    spec = pl.pallas_call(
-        functools.partial(filter_kernel, length, count, STEP_BLOCKS),
-        in_specs=[vmem] * 5 + [hbm, hbm] + [vmem] * 3,
-        out_specs=vmem,
-        out_shape=pltpu.VMEM((groups, count * blocks, 2 * span), BF16),
-        scratch_shapes=[
-            pltpu.VMEM((blocks * channels, span), F32),
-            pltpu.VMEM((channels, span), F32),
-            pltpu.VMEM((2 * blocks, lanes), F32),
-            pltpu.VMEM((lanes, 2 * blocks), F32),
-            pltpu.SemaphoreType.DMA((2,)),
-        ],
-        cost_estimate=pl.CostEstimate(
-            flops=20_000_000_000, bytes_accessed=2_000_000, transcendentals=2_000_000
-        ),
-        compiler_params=params(12),
-        name="filter",
-    )(
-        pos_weight,
-        pos_bias[None],
-        inner_weight,
-        inner_bias,
-        frequency[None],
-        out_weight,
-        decay_rates[None],
-        first,
-        twiddle,
-        forward,
-    )
+    shape = pltpu.VMEM((groups, count * blocks, 2 * span), BF16)
+
+    def filter_spectrum(turn, held):
+        def call(*args):
+            return filter_kernel(turn, held is not None, length, count, STEP_BLOCKS, *args)
+
+        return pl.pallas_call(
+            call,
+            in_specs=[vmem] * 5 + [hbm, hbm] + [vmem] * (3 if held is None else 4),
+            out_specs=vmem,
+            out_shape=shape,
+            input_output_aliases={} if held is None else {10: 0},
+            scratch_shapes=[
+                pltpu.VMEM((blocks * channels, span), F32),
+                pltpu.VMEM((channels, span), F32),
+                pltpu.VMEM((2 * blocks, lanes), F32),
+                pltpu.VMEM((lanes, 2 * blocks), F32),
+                pltpu.SemaphoreType.DMA((2,)),
+            ],
+            cost_estimate=pl.CostEstimate(
+                flops=20_000_000_000, bytes_accessed=2_000_000, transcendentals=2_000_000
+            ),
+            compiler_params=params(24),
+            name=f"filter{turn}",
+        )(
+            pos_weight,
+            pos_bias[None],
+            inner_weight,
+            inner_bias,
+            frequency[None],
+            out_weight,
+            decay_rates[None],
+            first,
+            twiddle,
+            forward,
+            *(() if held is None else (held,)),
+        )
+
+    early = filter_spectrum(EARLY, None)
+    gated, early = lax.optimization_barrier((gated, early))
+    arrived = exchange(gated.reshape(blocks, channels, span))
+    spec = filter_spectrum(1 - EARLY, early)
 
     convolved = pl.pallas_call(
         functools.partial(convolve_kernel, count),
@@ -402,11 +455,11 @@
             pltpu.VMEM((blocks * channels, span), F32),
             pltpu.VMEM((blocks * channels, span), F32),
         ],
-        compiler_params=params(12),
+        compiler_params=params(24),
         name="convolve",
-    )(arrived, spec, first, last, twiddle, forward, backward)
-
-    returned = lax.all_to_all(convolved, "seq", split_axis=0, concat_axis=0, tiled=True)
+    )(arrived, spec, first_data, last, twiddle, forward, backward)
+
+    returned = exchange(convolved)
 
     signal, gate_in, gate_out, _ = lax.optimization_barrier(
         (signal, gate_in, gate_out, convolved)

time: 72.8 us -> 59.7 us (0.82)
  the two profiles are of different devices: /device:TPU:32 before, /device:TPU:7 now
where the time goes in v3:
time: 59.7 us; the launch traced here: 59.3 us
  starting transfers between devices  25.2 us (42%)
  waiting for transfers between devices  17.4 us (29%)
  Pallas kernels  14.8 us (25%)
  local copies, waits for them, and re-layouts  1.69 us (3%)
    all_to_all x1, starting transfers between devices, per_device(): arrived = exchange(gated.reshape(blocks, channels, span))  14.7 us
    all_to_all x1, starting transfers between devices, per_device(): returned = exchange(convolved)  10.5 us
    all_to_all x1, waiting for transfers between devices, per_device(): arrived = exchange(gated.reshape(blocks, channels, span))  9.08 us
    pallas_call x2, Pallas kernels, filter_spectrum(): pl.pallas_call(call, in_specs=[vmem] * 5 + [hbm, hbm] + [vmem] * (3 if he...  8.34 us
    all_to_all x1, waiting for transfers between devices, per_device(): returned = exchange(convolved)  8.29 us
    pallas_call x1, Pallas kernels, per_device(): pl.pallas_call(functools.partial(convolve_kernel, count), in_specs=[vmem]...  3.17 us
    pallas_call x1, Pallas kernels, per_device(): pl.pallas_call(functools.partial(gate_kernel, chunk), in_specs=[hbm, hbm]...  2.22 us
    unnamed x34, local copies, waits for them, and re-layouts  1.69 us
  transfers between devices with their start and end apart: 2, of which 2 were waited for; matrix products, arithmetic and copies ran while one was open for 0% of the time, Pallas kernels for 0%

profile of v3, /device:TPU:7, one launch (start us, length us, event | category | flops | bytes accessed | tf_op | source)
XLA Modules:
  0.0 59.3 jit_solution(8013077719994088820)
XLA Ops:
  0.0 0.0 copy-start.9
  0.0 0.0 copy-start.10
  0.0 0.0 copy-start.11
  0.0 0.0 copy-start.15
  0.0 0.0 copy-start.16
  0.1 2.2 %gate.1 = bf16[2048,128]{1,0:T(8,128)(2,1)} custom-call(bf16[128,2048]{1,0:T(8,128)(2,1)} %bitcast.11, bf16[128,2048]{1,0:T(8,128)(2,1)} %bitcast.13), custom_call_target="tpu_custom_call" | custom-call | tf_op jit(solution)/shard_map/gate/pallas_call | solution.py:389
  2.3 0.0 copy-start.13
  2.3 0.0 copy-start.14
  2.3 0.0 copy-done.2
  2.3 0.0 copy-done.4
  2.3 0.0 copy-done.7
  2.3 0.0 copy-done.9
  2.4 0.6 copy-done.13
  3.0 8.3 %filter1.1.args_10_ = bf16[2,1024,256]{2,1,0:T(8,128)(2,1)S(1)} custom-call(f32[33,64]{1,0:T(8,128)S(1)} %copy-done.10, f32[1,64]{1,0:T(1,128)S(1)} %bitcast.19, f32[2,64,64]{2,1,0:T(8,128)S(1)} %copy-done.9, f32[2,64]{1,0:T(2,128)S(1)} %copy-done.13, f32[1,64]{1,0:T(1,128)S(1)} %bitcast.21, f32[64,2048]{1,0:T(8,128)S(1)} %copy-done.7, ...), custom_call_target="tpu_custom_call" | custom-call | flops 20000000000 | bytes 2000000 | tf_op jit(solution)/shard_map/filter1/pallas_call | solution.py:412
  11.3 14.7 %all-to-all-start = ((bf16[64,32,128]{2,1,0:T(8,128)(2,1)}), bf16[64,32,128]{2,1,0:T(8,128)(2,1)S(1)}, u32[]{:S(2)}, u32[]{:S(2)}) async-start(bf16[64,32,128]{2,1,0:T(8,128)(2,1)} %bitcast.5), calls=%async_computation | async-start | bytes 1048576 | tf_op jit(solution)/shard_map/all_to_all | solution.py:446
  26.0 0.0 copy-start.3
  26.0 0.0 copy-start.5
  26.0 0.0 copy-start.6
  26.1 9.1 %all-to-all-done.data_ref = bf16[64,32,128]{2,1,0:T(8,128)(2,1)S(1)} async-done(((bf16[64,32,128]{2,1,0:T(8,128)(2,1)}), bf16[64,32,128]{2,1,0:T(8,128)(2,1)S(1)}, u32[]{:S(2)}, u32[]{:S(2)}) %all-to-all-start) | async-done | bytes 524320 | tf_op jit(solution)/shard_map/all_to_all | solution.py:446
  35.2 0.0 copy-done.3
  35.2 0.0 copy-done.6
  35.2 0.0 copy-start.12
  35.2 3.2 %convolve.1 = bf16[64,32,128]{2,1,0:T(8,128)(2,1)} custom-call(bf16[64,32,128]{2,1,0:T(8,128)(2,1)S(1)} %all-to-all-done.data_ref, bf16[2,1024,256]{2,1,0:T(8,128)(2,1)S(1)} %filter0.1.spec_ref, bf16[128,64]{1,0:T(8,128)(2,1)S(1)} %copy-done.5, bf16[64,128]{1,0:T(8,128)(2,1)S(1)} %copy-done.6, f32[2,64,128]{2,1,0:T(8,128)S(1)} %copy-done.4, ...), custom_call_target="tpu_custom_call" | custom-call | tf_op jit(solution)/shard_map/convolve/pallas_call | solution.py:449
  38.4 10.5 %all-to-all-start.1 = ((bf16[64,32,128]{2,1,0:T(8,128)(2,1)}), bf16[64,32,128]{2,1,0:T(8,128)(2,1)S(1)}, u32[]{:S(2)}, u32[]{:S(2)}) async-start(bf16[64,32,128]{2,1,0:T(8,128)(2,1)} %convolve.1), calls=%async_computation.1 | async-start | bytes 1048576 | tf_op jit(solution)/shard_map/all_to_all | solution.py:462
  48.9 0.0 copy-done.12
  48.9 0.0 copy-done
  48.9 0.0 copy-done.1
  48.9 0.0 copy-start.8
  48.9 1.0 %copy-done.8 = bf16[1,128,2048]{2,1,0:T(8,128)(2,1)S(1)} copy-done((bf16[1,128,2048]{2,1,0:T(8,128)(2,1)S(1)}, bf16[1,128,2048]{2,1,0:T(8,128)(2,1)}, u32[]{:S(2)}) %copy-start.8) | copy-done | bytes 524312
  49.9 0.2 stage.1
  50.1 8.3 %all-to-all-done.1 = bf16[64,32,128]{2,1,0:T(8,128)(2,1)S(1)} async-done(((bf16[64,32,128]{2,1,0:T(8,128)(2,1)}), bf16[64,32,128]{2,1,0:T(8,128)(2,1)S(1)}, u32[]{:S(2)}, u32[]{:S(2)}) %all-to-all-start.1) | async-done | bytes 524320 | tf_op jit(solution)/shard_map/all_to_all | solution.py:462
  58.4 0.9 %mix.1 = bf16[128,2048]{1,0:T(8,128)(2,1)} custom-call(bf16[2048,128]{1,0:T(8,128)(2,1)S(1)} %bitcast.10, f32[128,2048]{1,0:T(8,128)S(1)} %get-tuple-element.17.direct_ref, bf16[128,2048]{1,0:T(8,128)(2,1)S(1)} %get-tuple-element.18.held_ref), custom_call_target="tpu_custom_call" | custom-call | tf_op jit(solution)/shard_map/mix/pallas_call | solution.py:479
  (12 shorter events, 0.1 us)
Async XLA Ops:
  0.0 2.3 %copy-start.2 = (bf16[256,256]{1,0:T(8,128)(2,1)S(1)}, bf16[256,256]{1,0:T(8,128)(2,1)}, u32[]{:S(2)}) copy-start(bf16[256,256]{1,0:T(8,128)(2,1)} %constant.19.clone.args_9_.forward_ref) | copy-start | bytes 393220
  0.0 2.3 %copy-start.4 = (f32[2,64,128]{2,1,0:T(8,128)S(1)}, f32[2,64,128]{2,1,0:T(8,128)}, u32[]{:S(2)}) copy-start(f32[2,64,128]{2,1,0:T(8,128)} %constant.18.clone.args_8_.twiddle_ref) | copy-start | bytes 196612
  0.0 2.3 %copy-start.7 = (f32[64,2048]{1,0:T(8,128)S(1)}, f32[64,2048]{1,0:T(8,128)}, u32[]{:S(2)}) copy-start(f32[64,2048]{1,0:T(8,128)} %args_5_.6) | copy-start | bytes 1572868
  0.0 2.3 %copy-start.9 = (f32[2,64,64]{2,1,0:T(8,128)S(1)}, f32[2,64,64]{2,1,0:T(8,128)}, u32[]{:S(2)}) copy-start(f32[2,64,64]{2,1,0:T(8,128)} %args_2_.6) | copy-start | bytes 98308
  0.0 2.3 %copy-start.10 = (f32[33,64]{1,0:T(8,128)S(1)}, f32[33,64]{1,0:T(8,128)}, u32[]{:S(2)}) copy-start(f32[33,64]{1,0:T(8,128)} %args_0_.6) | copy-start | bytes 25348
  0.0 2.3 %copy-start.11 = (f32[2048]{0:T(1024)S(1)}, f32[2048]{0:T(1024)}, u32[]{:S(2)}) copy-start(f32[2048]{0:T(1024)} %param.28) | copy-start | bytes 24580
  0.0 2.3 %copy-start.15 = (f32[64]{0:T(128)S(1)}, f32[64]{0:T(128)}, u32[]{:S(2)}) copy-start(f32[64]{0:T(128)} %param.26) | copy-start | bytes 772
  0.0 2.3 %copy-start.16 = (bf16[128,64]{1,0:T(8,128)(2,1)S(1)}, bf16[128,64]{1,0:T(8,128)(2,1)}, u32[]{:S(2)}) copy-start(bf16[128,64]{1,0:T(8,128)(2,1)} %constant.16.clone.args_7_) | copy-start | bytes 49156
  2.3 0.7 %copy-start.13 = (f32[2,64]{1,0:T(2,128)S(1)}, f32[2,64]{1,0:T(2,128)}, u32[]{:S(2)}) copy-start(f32[2,64]{1,0:T(2,128)} %args_3_.6) | copy-start | bytes 1540
  2.3 0.7 %copy-start.14 = (f32[64]{0:T(128)S(1)}, f32[64]{0:T(128)}, u32[]{:S(2)}) copy-start(f32[64]{0:T(128)} %param.23) | copy-start | bytes 772
  11.3 23.9 %all-to-all-start = ((bf16[64,32,128]{2,1,0:T(8,128)(2,1)}), bf16[64,32,128]{2,1,0:T(8,128)(2,1)S(1)}, u32[]{:S(2)}, u32[]{:S(2)}) async-start(bf16[64,32,128]{2,1,0:T(8,128)(2,1)} %bitcast.5), calls=%async_computation | async-start | bytes 1048576 | tf_op jit(solution)/shard_map/all_to_all | solution.py:446
  26.0 9.2 %copy-start.3 = (bf16[256,256]{1,0:T(8,128)(2,1)S(1)}, bf16[256,256]{1,0:T(8,128)(2,1)}, u32[]{:S(2)}) copy-start(bf16[256,256]{1,0:T(8,128)(2,1)} %constant.20.clone.backward_ref) | copy-start | bytes 393220
  26.0 9.2 %copy-start.5 = (bf16[128,64]{1,0:T(8,128)(2,1)S(1)}, bf16[128,64]{1,0:T(8,128)(2,1)}, u32[]{:S(2)}) copy-start(bf16[128,64]{1,0:T(8,128)(2,1)} %constant.27.first_ref) | copy-start | bytes 49156
  26.0 9.2 %copy-start.6 = (bf16[64,128]{1,0:T(8,128)(2,1)S(1)}, bf16[64,128]{1,0:T(8,128)(2,1)}, u32[]{:S(2)}) copy-start(bf16[64,128]{1,0:T(8,128)(2,1)} %constant.28.last_ref) | copy-start | bytes 49156
  35.2 13.7 %copy-start.12 = (f32[2048]{0:T(1024)S(1)}, f32[2048]{0:T(1024)}, u32[]{:S(2)}) copy-start(f32[2048]{0:T(1024)} %param.29) | copy-start | bytes 24580
  38.4 10.5 %copy-start = (bf16[1,128,2048]{2,1,0:T(8,128)(2,1)S(1)}, bf16[1,128,2048]{2,1,0:T(8,128)(2,1)}, u32[]{:S(2)}) copy-start(bf16[1,128,2048]{2,1,0:T(8,128)(2,1)} %param.19) | copy-start | bytes 1572868
  38.4 10.5 %copy-start.1 = (bf16[1,128,2048]{2,1,0:T(8,128)(2,1)S(1)}, bf16[1,128,2048]{2,1,0:T(8,128)(2,1)}, u32[]{:S(2)}) copy-start(bf16[1,128,2048]{2,1,0:T(8,128)(2,1)} %param.20) | copy-start | bytes 1572868
  38.4 20.0 %all-to-all-start.1 = ((bf16[64,32,128]{2,1,0:T(8,128)(2,1)}), bf16[64,32,128]{2,1,0:T(8,128)(2,1)S(1)}, u32[]{:S(2)}, u32[]{:S(2)}) async-start(bf16[64,32,128]{2,1,0:T(8,128)(2,1)} %convolve.1), calls=%async_computation.1 | async-start | bytes 1048576 | tf_op jit(solution)/shard_map/all_to_all | solution.py:462
  48.9 1.0 %copy-start.8 = (bf16[1,128,2048]{2,1,0:T(8,128)(2,1)S(1)}, bf16[1,128,2048]{2,1,0:T(8,128)(2,1)}, u32[]{:S(2)}) copy-start(bf16[1,128,2048]{2,1,0:T(8,128)(2,1)} %param.21) | copy-start | bytes 1572868

commit v4 on v3

--- a/solution.py
+++ b/solution.py
@@ -15,7 +15,6 @@
 F32 = jnp.float32
 BF16 = jnp.bfloat16
 STEP_BLOCKS = 16
-UNROLL_GROUPS = 2
 EARLY = 1
 SINE = (
     6.283182818534707,
@@ -156,7 +155,6 @@
 
 def filter_body(
     total,
-    count,
     step_blocks,
     pos_weight_ref,
     pos_bias_ref,
@@ -165,10 +163,6 @@
     frequency_ref,
     out_weight_hbm,
     decay_hbm,
-    first_ref,
-    twiddle_ref,
-    forward_ref,
-    spec_ref,
     taps_ref,
     square_ref,
     own_ref,
@@ -244,29 +238,36 @@
     summed = jnp.sum(square_ref[...], axis=1, keepdims=True)
     square_ref[...] = jnp.broadcast_to(lax.rsqrt(summed + EPSILON), square_ref.shape)
 
-    def spectrum_step(group, carry):
+
+def filter_kernel(turn, total, step_blocks, *refs):
+    own_turn = lax.axis_index("grp") % 2 == turn
+    if len(refs) > 12:
+        held_taps_ref, held_scale_ref, taps_ref, scale_ref = refs[7:11]
+        refs = refs[:7] + refs[9:]
+
+        @pl.when(jnp.logical_not(own_turn))
+        def _():
+            taps_ref[...] = held_taps_ref[...]
+            scale_ref[...] = held_scale_ref[...]
+
+    @pl.when(own_turn)
+    def _():
+        filter_body(total, step_blocks, *refs)
+
+
+def spectrum_kernel(count, taps_ref, scale_ref, first_ref, twiddle_ref, forward_ref, spec_ref):
+    channels = scale_ref.shape[0]
+    blocks = taps_ref.shape[0] // channels
+    for group in range(channels // count):
         spectrum = spectrum_of(
             taps_ref, group, count, blocks, channels, first_ref[...], twiddle_ref, forward_ref[...]
         )
         pieces = []
         for j in range(count):
-            scale = square_ref[pl.ds(group * count + j, 1), :]
+            scale = scale_ref[pl.ds(group * count + j, 1), :]
             scale = jnp.concatenate([scale, scale], axis=1)
             pieces.append((spectrum[j * blocks : (j + 1) * blocks] * scale).astype(BF16))
         spec_ref[group] = jnp.concatenate(pieces, axis=0)
-        return carry
-
-    lax.fori_loop(0, channels // count, spectrum_step, 0, unroll=UNROLL_GROUPS)
-
-
-def filter_kernel(turn, held, *args):
-    scalars, refs = args[:3], args[3:]
-    if held:
-        refs = refs[:10] + refs[11:]
-
-    @pl.when(lax.axis_index("grp") % 2 == turn)
-    def _():
-        filter_body(*scalars, *refs)
 
 
 def convolve_kernel(
@@ -278,14 +279,16 @@
     twiddle_ref,
     forward_ref,
     backward_ref,
-    out_ref,
+    out_hbm,
     rows_ref,
     result_ref,
+    out_ref,
+    sems,
 ):
     blocks, channels, span = data_ref.shape
     rows_ref[...] = data_ref[...].astype(F32).reshape(blocks * channels, span)
-
-    def group_step(group, carry):
+    copies = []
+    for group in range(channels // count):
         spectrum = spectrum_of(
             rows_ref, group, count, blocks, channels, first_ref[...], twiddle_ref, forward_ref[...]
         )
@@ -318,13 +321,15 @@
             last_ref[...], jnp.concatenate(turned, axis=1), preferred_element_type=F32
         )
         for j in range(count):
-            result_ref[pl.ds(group * count + j, blocks, stride=channels), :] = convolved[
-                :, j * span : (j + 1) * span
-            ]
-        return carry
-
-    lax.fori_loop(0, channels // count, group_step, 0, unroll=UNROLL_GROUPS)
-    out_ref[...] = result_ref[...].reshape(blocks, channels, span).astype(BF16)
+            result_ref[pl.ds(j, blocks, stride=count), :] = convolved[:, j * span : (j + 1) * span]
+        at = pl.ds(group * count, count)
+        out_ref[:, at, :] = result_ref[...].reshape(blocks, count, span).astype(BF16)
+        copies.append(
+            pltpu.make_async_copy(out_ref.at[:, at, :], out_hbm.at[:, at, :], sems.at[group])
+        )
+        copies[-1].start()
+    for copy in copies:
+        copy.wait()
 
 
 def stage_kernel(signal_ref, gate_ref, out_gate_ref, skip_ref, direct_ref, held_ref):
@@ -398,26 +403,35 @@
             pltpu.SemaphoreType.DMA((2, chunks)),
             pltpu.SemaphoreType.DMA((chunks,)),
         ],
+        cost_estimate=pl.CostEstimate(
+            flops=3_000_000_000, bytes_accessed=2_000_000, transcendentals=0
+        ),
         compiler_params=params(60),
         name="gate",
     )(signal, gate_in)
 
     lanes = span
-    shape = pltpu.VMEM((groups, count * blocks, 2 * span), BF16)
-
-    def filter_spectrum(turn, held):
-        def call(*args):
-            return filter_kernel(turn, held is not None, length, count, STEP_BLOCKS, *args)
-
+    network = (
+        pos_weight,
+        pos_bias[None],
+        inner_weight,
+        inner_bias,
+        frequency[None],
+        out_weight,
+        decay_rates[None],
+    )
+
+    def filter_taps(turn, held):
         return pl.pallas_call(
-            call,
-            in_specs=[vmem] * 5 + [hbm, hbm] + [vmem] * (3 if held is None else 4),
-            out_specs=vmem,
-            out_shape=shape,
-            input_output_aliases={} if held is None else {10: 0},
-            scratch_shapes=[
+            functools.partial(filter_kernel, turn, length, STEP_BLOCKS),
+            in_specs=[vmem] * 5 + [hbm, hbm] + [vmem] * len(held),
+            out_specs=[vmem] * 2,
+            out_shape=[
                 pltpu.VMEM((blocks * channels, span), F32),
                 pltpu.VMEM((channels, span), F32),
+            ],
+            input_output_aliases={7: 0, 8: 1} if held else {},
+            scratch_shapes=[
                 pltpu.VMEM((2 * blocks, lanes), F32),
                 pltpu.VMEM((lanes, 2 * blocks), F32),
                 pltpu.SemaphoreType.DMA((2,)),
@@ -427,33 +441,34 @@
             ),
             compiler_params=params(24),
             name=f"filter{turn}",
-        )(
-            pos_weight,
-            pos_bias[None],
-            inner_weight,
-            inner_bias,
-            frequency[None],
-            out_weight,
-            decay_rates[None],
-            first,
-            twiddle,
-            forward,
-            *(() if held is None else (held,)),
-        )
-
-    early = filter_spectrum(EARLY, None)
-    gated, early = lax.optimization_barrier((gated, early))
+        )(*network, *held)
+
+    taps, scale = filter_taps(EARLY, ())
+    gated, scale = lax.optimization_barrier((gated, scale))
     arrived = exchange(gated.reshape(blocks, channels, span))
-    spec = filter_spectrum(1 - EARLY, early)
+    taps, scale = filter_taps(1 - EARLY, (taps, scale))
+    spec = pl.pallas_call(
+        functools.partial(spectrum_kernel, count),
+        in_specs=[vmem] * 5,
+        out_specs=vmem,
+        out_shape=pltpu.VMEM((groups, count * blocks, 2 * span), BF16),
+        cost_estimate=pl.CostEstimate(
+            flops=2_000_000_000, bytes_accessed=2_000_000, transcendentals=0
+        ),
+        compiler_params=params(16),
+        name="spectrum",
+    )(taps, scale, first, twiddle, forward)
 
     convolved = pl.pallas_call(
         functools.partial(convolve_kernel, count),
         in_specs=[vmem] * 7,
-        out_specs=vmem,
-        out_shape=pltpu.VMEM((blocks, channels, span), BF16),
+        out_specs=hbm,
+        out_shape=jax.ShapeDtypeStruct((blocks, channels, span), BF16),
         scratch_shapes=[
             pltpu.VMEM((blocks * channels, span), F32),
-            pltpu.VMEM((blocks * channels, span), F32),
+            pltpu.VMEM((blocks * count, span), F32),
+            pltpu.VMEM((blocks, channels, span), BF16),
+            pltpu.SemaphoreType.DMA((groups,)),
         ],
         compiler_params=params(24),
         name="convolve",

time: 59.7 us -> 59.4 us (level)
  waiting for transfers between devices: 17.4 us -> 16.3 us
  local copies, waits for them, and re-layouts: 1.69 us -> 2.41 us
    all_to_all x1, waiting for transfers between devices: 9.08 us -> 7.04 us  [per_device(): arrived = exchange(gated.reshape(blocks, channels, span))]
    all_to_all x1, waiting for transfers between devices: 8.29 us -> 9.3 us  [per_device(): returned = exchange(convolved)]
    unnamed x34, local copies, waits for them, and re-layouts: 1.69 us -> 2.41 us
    pallas_call x2 -> x3, Pallas kernels: 8.34 us -> 8.55 us  [the longest x2 7.41 us: filter_taps(): pl.pallas_call(functools.partial(filter_kernel, turn, length, STEP_BLOCKS...]
  transfers between devices with their start and end apart: 2 -> 2, of which waited for: 2 -> 2; matrix products, arithmetic and copies ran while one was open for 0% -> 0% of each run, Pallas kernels for 0% -> 3%
where the time goes in v4:
time: 59.4 us; the launch traced here: 59.1 us
  starting transfers between devices  25.4 us (43%)
  waiting for transfers between devices  16.3 us (27%)
  Pallas kernels  14.7 us (25%)
  local copies, waits for them, and re-layouts  2.41 us (4%)
    all_to_all x1, starting transfers between devices, per_device(): arrived = exchange(gated.reshape(blocks, channels, span))  14.7 us
    all_to_all x1, starting transfers between devices, per_device(): returned = exchange(convolved)  10.7 us
    all_to_all x1, waiting for transfers between devices, per_device(): returned = exchange(convolved)  9.3 us
    pallas_call x2, Pallas kernels, filter_taps(): pl.pallas_call(functools.partial(filter_kernel, turn, length, STEP_BLOCKS...  7.41 us
    all_to_all x1, waiting for transfers between devices, per_device(): arrived = exchange(gated.reshape(blocks, channels, span))  7.04 us
    pallas_call x1, Pallas kernels, per_device(): pl.pallas_call(functools.partial(convolve_kernel, count), in_specs=[vmem]...  2.77 us
    unnamed x34, local copies, waits for them, and re-layouts  2.41 us
    pallas_call x1, Pallas kernels, per_device(): pl.pallas_call(functools.partial(gate_kernel, chunk), in_specs=[hbm, hbm]...  2.21 us
  transfers between devices with their start and end apart: 2, of which 2 were waited for; matrix products, arithmetic and copies ran while one was open for 0% of the time, Pallas kernels for 3%

profile of v4, /device:TPU:7, one launch (start us, length us, event | category | flops | bytes accessed | tf_op | source)
XLA Modules:
  0.0 59.1 jit_solution(522736602104158776)
XLA Ops:
  0.0 0.0 copy-start.11
  0.0 0.0 copy-start.15
  0.0 2.2 %gate.1 = bf16[2048,128]{1,0:T(8,128)(2,1)} custom-call(bf16[128,2048]{1,0:T(8,128)(2,1)} %bitcast.11, bf16[128,2048]{1,0:T(8,128)(2,1)} %bitcast.13), custom_call_target="tpu_custom_call" | custom-call | flops 3000000000 | bytes 2000000 | tf_op jit(solution)/shard_map/gate/pallas_call | solution.py:394
  2.2 0.0 copy-start.13
  2.3 0.0 copy-start.14
  2.3 0.0 copy-done.5
  2.3 0.0 copy-done.9
  2.3 0.0 copy-done.10
  2.3 0.0 copy-done.11
  2.3 0.0 copy-done.15
  2.3 0.6 %copy-done.13 = f32[2,64]{1,0:T(2,128)S(1)} copy-done((f32[2,64]{1,0:T(2,128)S(1)}, f32[2,64]{1,0:T(2,128)}, u32[]{:S(2)}) %copy-start.13) | copy-done | bytes 536
  2.9 0.0 copy-done.14
  2.9 7.2 %filter1.1 = (f32[2048,128]{1,0:T(8,128)S(1)}, f32[32,128]{1,0:T(8,128)S(1)}) custom-call(f32[33,64]{1,0:T(8,128)S(1)} %copy-done.10, f32[1,64]{1,0:T(1,128)S(1)} %bitcast.19, f32[2,64,64]{2,1,0:T(8,128)S(1)} %copy-done.9, f32[2,64]{1,0:T(2,128)S(1)} %copy-done.13, f32[1,64]{1,0:T(1,128)S(1)} %bitcast.21, f32[64,2048]{1,0:T(8,128)S(1)} %copy-done.5, ...), custom_call_target="tpu_custom_call" | custom-call | flops 20000000000 | bytes 2000000 | tf_op jit(solution)/shard_map/filter1/pallas_call | solution.py:425
  10.2 14.7 %all-to-all-start = ((bf16[64,32,128]{2,1,0:T(8,128)(2,1)}), bf16[64,32,128]{2,1,0:T(8,128)(2,1)S(1)}, u32[]{:S(2)}, u32[]{:S(2)}) async-start(bf16[64,32,128]{2,1,0:T(8,128)(2,1)} %bitcast.5), calls=%async_computation | async-start | bytes 1048576 | tf_op jit(solution)/shard_map/all_to_all | solution.py:448
  24.9 0.0 copy-start
  24.9 0.0 copy-start.2
  24.9 0.0 copy-start.16
  24.9 0.2 filter0.1
  25.1 0.7 %copy-done = bf16[256,256]{1,0:T(8,128)(2,1)S(1)} copy-done((bf16[256,256]{1,0:T(8,128)(2,1)S(1)}, bf16[256,256]{1,0:T(8,128)(2,1)}, u32[]{:S(2)}) %copy-start) | copy-done | bytes 131096
  25.8 0.0 copy-start.4
  25.8 1.1 %spectrum.1.spec_ref = bf16[2,1024,256]{2,1,0:T(8,128)(2,1)S(1)} custom-call(f32[2048,128]{1,0:T(8,128)S(1)} %get-tuple-element.20.taps_ref, f32[32,128]{1,0:T(8,128)S(1)} %get-tuple-element.21.scale_ref, bf16[128,64]{1,0:T(8,128)(2,1)S(1)} %copy-done.16, f32[2,64,128]{2,1,0:T(8,128)S(1)} %copy-done.2, bf16[256,256]{1,0:T(8,128)(2,1)S(1)} %copy-done), custom_call_target="tpu_custom_call" | custom-call | flops 2000000000 | bytes 2000000 | tf_op jit(solution)/shard_map/spectrum/pallas_call | solution.py:450
  27.0 7.0 %all-to-all-done.data_ref = bf16[64,32,128]{2,1,0:T(8,128)(2,1)S(1)} async-done(((bf16[64,32,128]{2,1,0:T(8,128)(2,1)}), bf16[64,32,128]{2,1,0:T(8,128)(2,1)S(1)}, u32[]{:S(2)}, u32[]{:S(2)}) %all-to-all-start) | async-done | bytes 524320 | tf_op jit(solution)/shard_map/all_to_all | solution.py:448
  34.0 0.0 copy-start.12
  34.1 2.8 %convolve.1 = bf16[64,32,128]{2,1,0:T(8,128)(2,1)} custom-call(bf16[64,32,128]{2,1,0:T(8,128)(2,1)S(1)} %all-to-all-done.data_ref, bf16[2,1024,256]{2,1,0:T(8,128)(2,1)S(1)} %spectrum.1.spec_ref, bf16[128,64]{1,0:T(8,128)(2,1)S(1)} %copy-done.3, bf16[64,128]{1,0:T(8,128)(2,1)S(1)} %copy-done.4, f32[2,64,128]{2,1,0:T(8,128)S(1)} %copy-done.2, ...), custom_call_target="tpu_custom_call" | custom-call | tf_op jit(solution)/shard_map/convolve/pallas_call | solution.py:462
  36.8 0.0 copy-start.6
  36.8 0.0 copy-start.7
  36.9 10.7 %all-to-all-start.1 = ((bf16[64,32,128]{2,1,0:T(8,128)(2,1)}), bf16[64,32,128]{2,1,0:T(8,128)(2,1)S(1)}, u32[]{:S(2)}, u32[]{:S(2)}) async-start(bf16[64,32,128]{2,1,0:T(8,128)(2,1)} %convolve.1), calls=%async_computation.1 | async-start | bytes 1048576 | tf_op jit(solution)/shard_map/all_to_all | solution.py:477
  47.6 0.0 copy-start.8
  47.6 1.0 %copy-done.8 = bf16[1,128,2048]{2,1,0:T(8,128)(2,1)S(1)} copy-done((bf16[1,128,2048]{2,1,0:T(8,128)(2,1)S(1)}, bf16[1,128,2048]{2,1,0:T(8,128)(2,1)}, u32[]{:S(2)}) %copy-start.8) | copy-done | bytes 524312
  48.6 0.2 stage.1
  48.9 9.3 %all-to-all-done.1 = bf16[64,32,128]{2,1,0:T(8,128)(2,1)S(1)} async-done(((bf16[64,32,128]{2,1,0:T(8,128)(2,1)}), bf16[64,32,128]{2,1,0:T(8,128)(2,1)S(1)}, u32[]{:S(2)}, u32[]{:S(2)}) %all-to-all-start.1) | async-done | bytes 524320 | tf_op jit(solution)/shard_map/all_to_all | solution.py:477
  58.2 0.9 %mix.1 = bf16[128,2048]{1,0:T(8,128)(2,1)} custom-call(bf16[2048,128]{1,0:T(8,128)(2,1)S(1)} %bitcast.10, f32[128,2048]{1,0:T(8,128)S(1)} %get-tuple-element.25.direct_ref, bf16[128,2048]{1,0:T(8,128)(2,1)S(1)} %get-tuple-element.26.held_ref), custom_call_target="tpu_custom_call" | custom-call | tf_op jit(solution)/shard_map/mix/pallas_call | solution.py:494
  (13 shorter events, 0.0 us)
Async XLA Ops:
  0.0 2.3 %copy-start.5 = (f32[64,2048]{1,0:T(8,128)S(1)}, f32[64,2048]{1,0:T(8,128)}, u32[]{:S(2)}) copy-start(f32[64,2048]{1,0:T(8,128)} %refs_5_.3) | copy-start | bytes 1572868
  0.0 2.3 %copy-start.9 = (f32[2,64,64]{2,1,0:T(8,128)S(1)}, f32[2,64,64]{2,1,0:T(8,128)}, u32[]{:S(2)}) copy-start(f32[2,64,64]{2,1,0:T(8,128)} %refs_2_.3) | copy-start | bytes 98308
  0.0 2.3 %copy-start.10 = (f32[33,64]{1,0:T(8,128)S(1)}, f32[33,64]{1,0:T(8,128)}, u32[]{:S(2)}) copy-start(f32[33,64]{1,0:T(8,128)} %refs_0_.3) | copy-start | bytes 25348
  0.0 2.3 %copy-start.11 = (f32[2048]{0:T(1024)S(1)}, f32[2048]{0:T(1024)}, u32[]{:S(2)}) copy-start(f32[2048]{0:T(1024)} %param.28) | copy-start | bytes 24580
  0.0 2.3 %copy-start.15 = (f32[64]{0:T(128)S(1)}, f32[64]{0:T(128)}, u32[]{:S(2)}) copy-start(f32[64]{0:T(128)} %param.26) | copy-start | bytes 772
  2.2 0.7 %copy-start.13 = (f32[2,64]{1,0:T(2,128)S(1)}, f32[2,64]{1,0:T(2,128)}, u32[]{:S(2)}) copy-start(f32[2,64]{1,0:T(2,128)} %refs_3_.3) | copy-start | bytes 1540
  2.3 0.7 %copy-start.14 = (f32[64]{0:T(128)S(1)}, f32[64]{0:T(128)}, u32[]{:S(2)}) copy-start(f32[64]{0:T(128)} %param.23) | copy-start | bytes 772
  10.2 23.9 %all-to-all-start = ((bf16[64,32,128]{2,1,0:T(8,128)(2,1)}), bf16[64,32,128]{2,1,0:T(8,128)(2,1)S(1)}, u32[]{:S(2)}, u32[]{:S(2)}) async-start(bf16[64,32,128]{2,1,0:T(8,128)(2,1)} %bitcast.5), calls=%async_computation | async-start | bytes 1048576 | tf_op jit(solution)/shard_map/all_to_all | solution.py:448
  24.9 0.9 %copy-start = (bf16[256,256]{1,0:T(8,128)(2,1)S(1)}, bf16[256,256]{1,0:T(8,128)(2,1)}, u32[]{:S(2)}) copy-start(bf16[256,256]{1,0:T(8,128)(2,1)} %constant.19.clone.forward_ref) | copy-start | bytes 393220
  24.9 0.9 %copy-start.2 = (f32[2,64,128]{2,1,0:T(8,128)S(1)}, f32[2,64,128]{2,1,0:T(8,128)}, u32[]{:S(2)}) copy-start(f32[2,64,128]{2,1,0:T(8,128)} %constant.18.clone.twiddle_ref) | copy-start | bytes 196612
  24.9 0.9 %copy-start.16 = (bf16[128,64]{1,0:T(8,128)(2,1)S(1)}, bf16[128,64]{1,0:T(8,128)(2,1)}, u32[]{:S(2)}) copy-start(bf16[128,64]{1,0:T(8,128)(2,1)} %constant.16.clone.first_ref) | copy-start | bytes 49156
  25.8 8.2 %copy-start.1 = (bf16[256,256]{1,0:T(8,128)(2,1)S(1)}, bf16[256,256]{1,0:T(8,128)(2,1)}, u32[]{:S(2)}) copy-start(bf16[256,256]{1,0:T(8,128)(2,1)} %constant.20.clone.backward_ref) | copy-start | bytes 393220
  25.8 8.2 %copy-start.3 = (bf16[128,64]{1,0:T(8,128)(2,1)S(1)}, bf16[128,64]{1,0:T(8,128)(2,1)}, u32[]{:S(2)}) copy-start(bf16[128,64]{1,0:T(8,128)(2,1)} %constant.27.first_ref) | copy-start | bytes 49156
  25.8 8.2 %copy-start.4 = (bf16[64,128]{1,0:T(8,128)(2,1)S(1)}, bf16[64,128]{1,0:T(8,128)(2,1)}, u32[]{:S(2)}) copy-start(bf16[64,128]{1,0:T(8,128)(2,1)} %constant.28.last_ref) | copy-start | bytes 49156
  34.0 13.5 %copy-start.12 = (f32[2048]{0:T(1024)S(1)}, f32[2048]{0:T(1024)}, u32[]{:S(2)}) copy-start(f32[2048]{0:T(1024)} %param.29) | copy-start | bytes 24580
  36.8 10.8 %copy-start.6 = (bf16[1,128,2048]{2,1,0:T(8,128)(2,1)S(1)}, bf16[1,128,2048]{2,1,0:T(8,128)(2,1)}, u32[]{:S(2)}) copy-start(bf16[1,128,2048]{2,1,0:T(8,128)(2,1)} %param.19) | copy-start | bytes 1572868
  36.8 10.7 %copy-start.7 = (bf16[1,128,2048]{2,1,0:T(8,128)(2,1)S(1)}, bf16[1,128,2048]{2,1,0:T(8,128)(2,1)}, u32[]{:S(2)}) copy-start(bf16[1,128,2048]{2,1,0:T(8,128)(2,1)} %param.20) | copy-start | bytes 1572868
  36.9 21.3 %all-to-all-start.1 = ((bf16[64,32,128]{2,1,0:T(8,128)(2,1)}), bf16[64,32,128]{2,1,0:T(8,128)(2,1)S(1)}, u32[]{:S(2)}, u32[]{:S(2)}) async-start(bf16[64,32,128]{2,1,0:T(8,128)(2,1)} %convolve.1), calls=%async_computation.1 | async-start | bytes 1048576 | tf_op jit(solution)/shard_map/all_to_all | solution.py:477
  47.6 1.0 %copy-start.8 = (bf16[1,128,2048]{2,1,0:T(8,128)(2,1)S(1)}, bf16[1,128,2048]{2,1,0:T(8,128)(2,1)}, u32[]{:S(2)}) copy-start(bf16[1,128,2048]{2,1,0:T(8,128)(2,1)} %param.21) | copy-start | bytes 1572868
